TPU v7x, 32 devices: a whole 2x2x4 slice. The times are simulated.
32 devices in a mesh: seq: 8 (over z, x), tp: 4 (over y, core).
Axes of the slice: x: 2, y: 2, z: 4, core: 2. Of those that a mesh axis runs over, the one named last changes fastest.
Arguments:
- inputs: bfloat16 [2, 2048, 2048], P(None, 'seq'), may hold values from -6 to 6
- cotangent: bfloat16 [2, 2048, 2048], P(None, 'seq'), may hold values from -6 to 6
- attn_gain: bfloat16 [2048], P('seq'), may hold values from 0.5 to 1.5
- w_query: bfloat16 [2048, 2048], P('seq', 'tp'), may hold values from -0.125 to 0.125
- w_key: bfloat16 [2048, 2048], P('seq', 'tp'), may hold values from -0.125 to 0.125
- w_value: bfloat16 [2048, 3456], P('seq', 'tp'), may hold values from -0.125 to 0.125
- w_gate: bfloat16 [2048, 3456], P('seq', 'tp'), may hold values from -0.125 to 0.125
- w_out: bfloat16 [3456, 2048], P('tp', 'seq'), may hold values from -0.15625 to 0.15625
- ffn_gain: bfloat16 [2048], P('seq'), may hold values from 0.5 to 1.5
- w_glu: bfloat16 [2048, 3456], P('seq', 'tp'), may hold values from -0.125 to 0.125
- w_up: bfloat16 [2048, 3456], P('seq', 'tp'), may hold values from -0.125 to 0.125
- w_down: bfloat16 [3456, 2048], P('tp', 'seq'), may hold values from -0.15625 to 0.15625
- decay_rate: float32 [8], P('tp'), may hold values from 0 to 0.032, as said below
Outputs:
- outputs: bfloat16 [2, 2048, 2048], P(None, 'seq')
- input_grad: float32 [2, 2048, 2048], P(None, 'seq')
- attngain_grad: float32 [2048], P('seq')
- query_grad: float32 [2048, 2048], P('seq', 'tp')
- key_grad: float32 [2048, 2048], P('seq', 'tp')
- value_grad: float32 [2048, 3456], P('seq', 'tp')
- gate_grad: float32 [2048, 3456], P('seq', 'tp')
- out_grad: float32 [3456, 2048], P('tp', 'seq')
- ffngain_grad: float32 [2048], P('seq')
- glu_grad: float32 [2048, 3456], P('seq', 'tp')
- up_grad: float32 [2048, 3456], P('seq', 'tp')
- down_grad: float32 [3456, 2048], P('tp', 'seq')
Inputs may be any that keep to these rules, and one draw needn't show every extreme that they name: `decay_rate`: each head's decay rate; positive.
All inputs are finite; a program needn't handle non-finite values.
Results may differ from a plain program's by a relative error of at most 0.03.
Values may be sent and summed in bfloat16 or wider, within the bound.
A program may use at most 256 MiB of HBM per device.

v0:
```python
import math
import jax
import jax.numpy as jnp
from jax import lax
from jax.sharding import PartitionSpec as P

KEY = 256
VAL = 432
EPS_LAYER = 1e-05
EPS_GROUP = 1e-06
MAXIMAL_ACCURACY = lax.Precision.HIGHEST


def passed_along(block, axis, distance):
    devices = range(lax.axis_size(axis))
    route = [(i - distance, i) for i in devices if i - distance in devices]
    return lax.ppermute(block, axis, route)


def normalize(values, epsilon):
    average = jnp.mean(values, axis=-1, keepdims=True)
    centred = values - average
    inv_std = lax.rsqrt(jnp.mean(centred * centred, axis=-1, keepdims=True) + epsilon)
    return (centred * inv_std, inv_std)


def normalize_back(upstream, normed, inv_std):
    return inv_std * (
        upstream
        - jnp.mean(upstream, axis=-1, keepdims=True)
        - normed * jnp.mean(upstream * normed, axis=-1, keepdims=True)
    )


def swish_parts(values):
    sigmoid = jax.nn.sigmoid(values)
    return (values * sigmoid, sigmoid * (1.0 + values * (1.0 - sigmoid)))


def rotary_tables(positions, width):
    half_width = width // 2
    fraction = jnp.arange(half_width, dtype=jnp.float32) / max(half_width - 1, 1)
    frequency = jnp.power(10000.0, -fraction)
    angles = positions[:, None] * frequency[None, :]
    cosine = jnp.concatenate([jnp.cos(angles), jnp.cos(angles)], axis=-1)[:, None, :]
    sine_table = jnp.concatenate([jnp.sin(angles), jnp.sin(angles)], axis=-1)[:, None, :]
    return (cosine, sine_table)


def rotate(values, cosine, sine_table):
    half_width = values.shape[-1] // 2
    turned = jnp.concatenate([-values[..., half_width:], values[..., :half_width]], axis=-1)
    return values * cosine + turned * sine_table


def rotate_back(upstream, cosine, sine_table):
    half_width = upstream.shape[-1] // 2
    scaled = upstream * sine_table
    turned = jnp.concatenate([scaled[..., half_width:], -scaled[..., :half_width]], axis=-1)
    return upstream * cosine + turned


def decay_tables(rates, length):
    offsets = jnp.arange(length, dtype=jnp.float32)
    distance = offsets[:, None] - offsets[None, :]
    decay_mask = jnp.where(
        distance[None] >= 0.0,
        jnp.exp(-rates[:, None, None] * jnp.maximum(distance, 0.0)[None]),
        0.0,
    )
    leading_decay = jnp.exp(-rates[None, :] * (offsets[:, None] + 1.0))
    trailing_decay = jnp.exp(-rates[None, :] * (length - 1.0 - offsets[:, None]))
    return (decay_mask, leading_decay, trailing_decay)


def block_summary(key_rotated, value_matrix_rows, trailing_decay):
    return jnp.einsum(
        "ysu,ysb->sub",
        key_rotated.astype(jnp.float32) * trailing_decay[:, :, None],
        value_matrix_rows.astype(jnp.float32),
        precision=MAXIMAL_ACCURACY,
    )


def block_weights(query_rotated, key_rotated, decay_mask):
    scores = jnp.einsum(
        "ihk,jhk->hij", query_rotated, key_rotated, preferred_element_type=jnp.float32
    )
    return (scores * decay_mask).astype(jnp.bfloat16)


def block_output(
    query_rotated, key_rotated, value_matrix_rows, incoming_state, decay_mask, leading_decay
):
    layer_weights = block_weights(query_rotated, key_rotated, decay_mask)
    inner = jnp.einsum(
        "hij,jhv->ihv", layer_weights, value_matrix_rows, preferred_element_type=jnp.float32
    )
    carried_state = jnp.einsum(
        "jnq,nqs->jns",
        query_rotated.astype(jnp.float32) * leading_decay[:, :, None],
        incoming_state,
        precision=MAXIMAL_ACCURACY,
    )
    return inner + carried_state


def state_grad_own(query_rotated, output_gradient, leading_decay):
    return jnp.einsum(
        "pxa,pxb->xab",
        query_rotated.astype(jnp.float32) * leading_decay[:, :, None],
        output_gradient.astype(jnp.float32),
        precision=MAXIMAL_ACCURACY,
    )


def block_backward(
    query_rotated,
    key_rotated,
    value_matrix_rows,
    incoming_state,
    state_gradient,
    output_gradient,
    decay_mask,
    leading_decay,
    trailing_decay,
):
    weight_gradients = (
        jnp.einsum(
            "ihv,jhv->hij", output_gradient, value_matrix_rows, preferred_element_type=jnp.float32
        )
        * decay_mask
    ).astype(jnp.bfloat16)
    layer_weights = block_weights(query_rotated, key_rotated, decay_mask)
    query_gradient = jnp.einsum(
        "pzg,gpe->zpe", weight_gradients, key_rotated, preferred_element_type=jnp.float32
    ) + leading_decay[:, :, None] * jnp.einsum(
        "wcr,cdr->wcd",
        output_gradient.astype(jnp.float32),
        incoming_state,
        precision=MAXIMAL_ACCURACY,
    )
    key_gradient = jnp.einsum(
        "zun,uzf->nzf", weight_gradients, query_rotated, preferred_element_type=jnp.float32
    ) + trailing_decay[:, :, None] * jnp.einsum(
        "crp,rnp->crn",
        value_matrix_rows.astype(jnp.float32),
        state_gradient,
        precision=MAXIMAL_ACCURACY,
    )
    value_gradient = jnp.einsum(
        "lpb,plz->blz", layer_weights, output_gradient, preferred_element_type=jnp.float32
    ) + trailing_decay[:, :, None] * jnp.einsum(
        "zmf,mfn->zmn", key_rotated.astype(jnp.float32), state_gradient, precision=MAXIMAL_ACCURACY
    )
    return (query_gradient, key_gradient, value_gradient)


def carry_states(whole_decay, summary):

    def advance(turn_index, carried_state):
        return passed_along(whole_decay * carried_state + summary, "seq", 1)

    return lax.fori_loop(0, lax.axis_size("seq") - 1, advance, jnp.zeros_like(summary))


def carry_back(whole_decay, own_grad):

    def retreat(turn_index, carried_state):
        return passed_along(whole_decay * carried_state + own_grad, "seq", -1)

    return lax.fori_loop(0, lax.axis_size("seq") - 1, retreat, jnp.zeros_like(own_grad))


def on_device(
    inputs,
    cotangent,
    attn_gain,
    w_query,
    w_key,
    w_value,
    w_gate,
    w_out,
    ffn_gain,
    w_glu,
    w_up,
    w_down,
    decay_rate,
):
    seq_count, tok_rows, model_width = inputs.shape
    row_count = seq_count * tok_rows
    local_heads = decay_rate.shape[0]
    gathered = (
        lax.all_gather(w_query, "seq", axis=0, tiled=True),
        lax.all_gather(w_key, "seq", axis=0, tiled=True),
        lax.all_gather(w_value, "seq", axis=0, tiled=True),
        lax.all_gather(w_gate, "seq", axis=0, tiled=True),
        lax.all_gather(w_out, "seq", axis=1, tiled=True),
        lax.all_gather(w_glu, "seq", axis=0, tiled=True),
        lax.all_gather(w_up, "seq", axis=0, tiled=True),
        lax.all_gather(w_down, "seq", axis=1, tiled=True),
        lax.all_gather(attn_gain, "seq", axis=0, tiled=True),
        lax.all_gather(ffn_gain, "seq", axis=0, tiled=True),
    )
    (
        full_query,
        full_key,
        full_value,
        full_gate,
        full_out,
        full_glu,
        full_up,
        full_down,
        full_attn_gain,
        full_ffn_gain,
    ) = gathered
    residual = inputs.astype(jnp.float32).reshape(row_count, model_width)
    normed_one, inv_one = normalize(residual, EPS_LAYER)
    attn_in = (normed_one * full_attn_gain.astype(jnp.float32)).astype(jnp.bfloat16)
    query_lin = jnp.dot(attn_in, full_query, preferred_element_type=jnp.float32)
    key_lin = jnp.dot(attn_in, full_key, preferred_element_type=jnp.float32)
    value_lin = jnp.dot(attn_in, full_value, preferred_element_type=jnp.float32)
    gate_lin = jnp.dot(attn_in, full_gate, preferred_element_type=jnp.float32)
    offset = (lax.axis_index("seq") * tok_rows).astype(jnp.float32)
    positions = offset + jnp.arange(tok_rows, dtype=jnp.float32)
    cosine, sine_table = rotary_tables(positions, KEY)
    key_scale = 1.0 / math.sqrt(KEY)
    query_rotated = rotate(
        query_lin.reshape(seq_count, tok_rows, local_heads, KEY), cosine, sine_table
    ).astype(jnp.bfloat16)
    key_rotated = (
        rotate(key_lin.reshape(seq_count, tok_rows, local_heads, KEY), cosine, sine_table)
        * key_scale
    ).astype(jnp.bfloat16)
    value_matrix_rows = value_lin.reshape(seq_count, tok_rows, local_heads, VAL).astype(
        jnp.bfloat16
    )
    decay_mask, leading_decay, trailing_decay = decay_tables(decay_rate, tok_rows)
    whole_decay = jnp.exp(-decay_rate * tok_rows)[:, None, None]
    summary = jax.vmap(block_summary, in_axes=(0, 0, None))(
        key_rotated, value_matrix_rows, trailing_decay
    )
    incoming_state = carry_states(whole_decay, summary)
    retained = jax.vmap(block_output, in_axes=(0, 0, 0, 0, None, None))(
        query_rotated, key_rotated, value_matrix_rows, incoming_state, decay_mask, leading_decay
    )
    group_normed, group_inv = normalize(retained, EPS_GROUP)
    gate_act, gate_slope = swish_parts(gate_lin)
    group_flat = group_normed.reshape(row_count, local_heads * VAL)
    mixed = (gate_act * group_flat).astype(jnp.bfloat16)
    attn_out = lax.psum(jnp.dot(mixed, full_out, preferred_element_type=jnp.float32), "tp")
    middle = residual + attn_out
    normed_two, inv_two = normalize(middle, EPS_LAYER)
    ffn_in = (normed_two * full_ffn_gain.astype(jnp.float32)).astype(jnp.bfloat16)
    glu_lin = jnp.dot(ffn_in, full_glu, preferred_element_type=jnp.float32)
    up_lin = jnp.dot(ffn_in, full_up, preferred_element_type=jnp.float32)
    glu_act, glu_slope = swish_parts(glu_lin)
    hidden = (glu_act * up_lin).astype(jnp.bfloat16)
    ffn_out = lax.psum(jnp.dot(hidden, full_down, preferred_element_type=jnp.float32), "tp")
    final = middle + ffn_out
    outputs = final.astype(jnp.bfloat16).reshape(seq_count, tok_rows, model_width)
    back_weights = (
        lax.all_gather(w_query, "seq", axis=0, tiled=True),
        lax.all_gather(w_key, "seq", axis=0, tiled=True),
        lax.all_gather(w_value, "seq", axis=0, tiled=True),
        lax.all_gather(w_gate, "seq", axis=0, tiled=True),
        lax.all_gather(w_out, "seq", axis=1, tiled=True),
        lax.all_gather(w_glu, "seq", axis=0, tiled=True),
        lax.all_gather(w_up, "seq", axis=0, tiled=True),
        lax.all_gather(w_down, "seq", axis=1, tiled=True),
        lax.all_gather(attn_gain, "seq", axis=0, tiled=True),
        lax.all_gather(ffn_gain, "seq", axis=0, tiled=True),
    )
    (
        back_query,
        back_key,
        back_value,
        back_gate,
        back_out,
        back_glu,
        back_up,
        back_down,
        back_attn_gain,
        back_ffn_gain,
    ) = back_weights
    cot_rows = cotangent.reshape(row_count, model_width)
    down_grad = jnp.dot(hidden.T, cot_rows, preferred_element_type=jnp.float32)
    grad_hidden = jnp.dot(cot_rows, back_down.T, preferred_element_type=jnp.float32)
    grad_glu = (grad_hidden * up_lin * glu_slope).astype(jnp.bfloat16)
    grad_up = (grad_hidden * glu_act).astype(jnp.bfloat16)
    glu_grad = jnp.dot(ffn_in.T, grad_glu, preferred_element_type=jnp.float32)
    up_grad = jnp.dot(ffn_in.T, grad_up, preferred_element_type=jnp.float32)
    grad_ffn_in = lax.psum(
        jnp.dot(grad_glu, back_glu.T, preferred_element_type=jnp.float32)
        + jnp.dot(grad_up, back_up.T, preferred_element_type=jnp.float32),
        "tp",
    )
    ffngain_grad = jnp.sum(grad_ffn_in * normed_two, axis=0)
    grad_middle = cot_rows.astype(jnp.float32) + normalize_back(
        grad_ffn_in * back_ffn_gain.astype(jnp.float32), normed_two, inv_two
    )
    grad_middle_bf = grad_middle.astype(jnp.bfloat16)
    out_grad = jnp.dot(mixed.T, grad_middle_bf, preferred_element_type=jnp.float32)
    grad_mixed = jnp.dot(grad_middle_bf, back_out.T, preferred_element_type=jnp.float32)
    grad_gate = (grad_mixed * group_flat * gate_slope).astype(jnp.bfloat16)
    grad_group = (grad_mixed * gate_act).reshape(seq_count, tok_rows, local_heads, VAL)
    grad_retained = normalize_back(grad_group, group_normed, group_inv).astype(jnp.bfloat16)
    own_grad = jax.vmap(state_grad_own, in_axes=(0, 0, None))(
        query_rotated, grad_retained, leading_decay
    )
    state_gradient = carry_back(whole_decay, own_grad)
    grad_qrot, grad_krot, grad_vrows = jax.vmap(
        block_backward, in_axes=(0, 0, 0, 0, 0, 0, None, None, None)
    )(
        query_rotated,
        key_rotated,
        value_matrix_rows,
        incoming_state,
        state_gradient,
        grad_retained,
        decay_mask,
        leading_decay,
        trailing_decay,
    )
    query_gradient = (
        rotate_back(grad_qrot, cosine, sine_table)
        .reshape(row_count, local_heads * KEY)
        .astype(jnp.bfloat16)
    )
    key_gradient = (
        (rotate_back(grad_krot, cosine, sine_table) * key_scale)
        .reshape(row_count, local_heads * KEY)
        .astype(jnp.bfloat16)
    )
    value_gradient = grad_vrows.reshape(row_count, local_heads * VAL).astype(jnp.bfloat16)
    query_grad = jnp.dot(attn_in.T, query_gradient, preferred_element_type=jnp.float32)
    key_grad = jnp.dot(attn_in.T, key_gradient, preferred_element_type=jnp.float32)
    value_grad = jnp.dot(attn_in.T, value_gradient, preferred_element_type=jnp.float32)
    gate_grad = jnp.dot(attn_in.T, grad_gate, preferred_element_type=jnp.float32)
    partial_in = (
        jnp.dot(query_gradient, back_query.T, preferred_element_type=jnp.float32)
        + jnp.dot(key_gradient, back_key.T, preferred_element_type=jnp.float32)
        + jnp.dot(value_gradient, back_value.T, preferred_element_type=jnp.float32)
        + jnp.dot(grad_gate, back_gate.T, preferred_element_type=jnp.float32)
    )
    grad_attn_in = lax.psum(partial_in, "tp")
    attngain_grad = jnp.sum(grad_attn_in * normed_one, axis=0)
    input_grad = grad_middle + normalize_back(
        grad_attn_in * back_attn_gain.astype(jnp.float32), normed_one, inv_one
    )
    input_out = input_grad.reshape(seq_count, tok_rows, model_width)
    reduced = (
        lax.psum_scatter(query_grad, "seq", scatter_dimension=0, tiled=True),
        lax.psum_scatter(key_grad, "seq", scatter_dimension=0, tiled=True),
        lax.psum_scatter(value_grad, "seq", scatter_dimension=0, tiled=True),
        lax.psum_scatter(gate_grad, "seq", scatter_dimension=0, tiled=True),
        lax.psum_scatter(out_grad, "seq", scatter_dimension=1, tiled=True),
        lax.psum_scatter(glu_grad, "seq", scatter_dimension=0, tiled=True),
        lax.psum_scatter(up_grad, "seq", scatter_dimension=0, tiled=True),
        lax.psum_scatter(down_grad, "seq", scatter_dimension=1, tiled=True),
        lax.psum_scatter(attngain_grad, "seq", scatter_dimension=0, tiled=True),
        lax.psum_scatter(ffngain_grad, "seq", scatter_dimension=0, tiled=True),
    )
    return (
        outputs,
        input_out,
        reduced[8],
        reduced[0],
        reduced[1],
        reduced[2],
        reduced[3],
        reduced[4],
        reduced[9],
        reduced[5],
        reduced[6],
        reduced[7],
    )


def solution(mesh):
    return jax.shard_map(
        on_device,
        mesh=mesh,
        in_specs=(
            P(None, "seq", None),
            P(None, "seq", None),
            P("seq"),
            P("seq", "tp"),
            P("seq", "tp"),
            P("seq", "tp"),
            P("seq", "tp"),
            P("tp", "seq"),
            P("seq"),
            P("seq", "tp"),
            P("seq", "tp"),
            P("tp", "seq"),
            P("tp"),
        ),
        out_specs=(
            P(None, "seq", None),
            P(None, "seq", None),
            P("seq"),
            P("seq", "tp"),
            P("seq", "tp"),
            P("seq", "tp"),
            P("seq", "tp"),
            P("tp", "seq"),
            P("seq"),
            P("seq", "tp"),
            P("seq", "tp"),
            P("tp", "seq"),
        ),
        check_vma=False,
    )
```

profile of v0, /device:TPU:0, one launch (start us, length us, event | category | flops | bytes accessed | tf_op | source)
XLA Modules:
  0.0 2463.8 jit_solution(17136700813776060130)
XLA Ops:
  10.8 22.4 all-gather
  39.4 22.7 all-gather.17.cloned.1.call-done
  62.1 3.9 copy.81
  66.0 45.9 %all-gather.15.cloned.1.call-done = bf16[2048,512]{1,0:T(8,128)(2,1)} async-done(((bf16[256,512]{1,0:T(8,128)(2,1)}), bf16[2048,512]{1,0:T(8,128)(2,1)}) %all-gather.15.cloned.1.call-update) | async-done | bytes 2097168 | tf_op jit(solution)/shard_map/all_gather | solution.py:194
  111.9 4.1 copy.80
  122.3 57.4 %all-gather.13.cloned.1.call-done = bf16[2048,864]{0,1:T(8,128)(2,1)} async-done(((bf16[256,864]{0,1:T(8,128)(2,1)}), bf16[2048,864]{0,1:T(8,128)(2,1)}) %all-gather.13.cloned.1.call-update) | async-done | bytes 3538960 | tf_op jit(solution)/shard_map/all_gather | solution.py:196
  179.7 4.0 fusion.27
  186.6 373.1 %while.20 = (s32[]{:T(128)}, f32[2,2,256,432]{2,3,1,0:T(8,128)S(1)}, f32[2]{0:T(128)S(1)}, f32[2,2,256,432]{2,3,1,0:T(8,128)S(1)}, s32[]{:T(128)}) while((s32[]{:T(128)}, f32[2,2,256,432]{2,3,1,0:T(8,128)S(1)}, f32[2]{0:T(128)S(1)}, f32[2,2,256,432]{2,3,1,0:T(8,128)S(1)}, s32[]{:T(128)}) %tuple.65), condition=%wide.region_3.4_spmd, body=%wide.region_2.3_spmd.sunk | while | flops 884738 | bytes 12386413 | solution.py:164
  188.2 3.5 collective-permute-start
  191.6 48.9 %collective-permute-done = f32[2,2,256,432]{2,3,1,0:T(8,128)S(1)} collective-permute-done((f32[2,2,256,432]{2,3,1,0:T(8,128)}, f32[2,2,256,432]{2,3,1,0:T(8,128)S(1)}, u32[]{:S(2)}, u32[]{:S(2)}) %collective-permute-start) | collective-permute-done | bytes 1769504 | tf_op jit(solution)/shard_map/while/body/eval_jaxpr/ppermute | solution.py:17
  242.2 23.1 collective-permute-start
  265.2 42.4 %collective-permute-done = f32[2,2,256,432]{2,3,1,0:T(8,128)S(1)} collective-permute-done((f32[2,2,256,432]{2,3,1,0:T(8,128)}, f32[2,2,256,432]{2,3,1,0:T(8,128)S(1)}, u32[]{:S(2)}, u32[]{:S(2)}) %collective-permute-start) | collective-permute-done | bytes 1769504 | tf_op jit(solution)/shard_map/while/body/eval_jaxpr/ppermute | solution.py:17
  309.3 18.4 collective-permute-start
  327.7 50.1 %collective-permute-done = f32[2,2,256,432]{2,3,1,0:T(8,128)S(1)} collective-permute-done((f32[2,2,256,432]{2,3,1,0:T(8,128)}, f32[2,2,256,432]{2,3,1,0:T(8,128)S(1)}, u32[]{:S(2)}, u32[]{:S(2)}) %collective-permute-start) | collective-permute-done | bytes 1769504 | tf_op jit(solution)/shard_map/while/body/eval_jaxpr/ppermute | solution.py:17
  379.3 13.7 collective-permute-start
  393.1 37.7 %collective-permute-done = f32[2,2,256,432]{2,3,1,0:T(8,128)S(1)} collective-permute-done((f32[2,2,256,432]{2,3,1,0:T(8,128)}, f32[2,2,256,432]{2,3,1,0:T(8,128)S(1)}, u32[]{:S(2)}, u32[]{:S(2)}) %collective-permute-start) | collective-permute-done | bytes 1769504 | tf_op jit(solution)/shard_map/while/body/eval_jaxpr/ppermute | solution.py:17
  432.3 5.3 collective-permute-start
  437.6 36.8 %collective-permute-done = f32[2,2,256,432]{2,3,1,0:T(8,128)S(1)} collective-permute-done((f32[2,2,256,432]{2,3,1,0:T(8,128)}, f32[2,2,256,432]{2,3,1,0:T(8,128)S(1)}, u32[]{:S(2)}, u32[]{:S(2)}) %collective-permute-start) | collective-permute-done | bytes 1769504 | tf_op jit(solution)/shard_map/while/body/eval_jaxpr/ppermute | solution.py:17
  476.0 5.3 collective-permute-start
  481.3 36.0 %collective-permute-done = f32[2,2,256,432]{2,3,1,0:T(8,128)S(1)} collective-permute-done((f32[2,2,256,432]{2,3,1,0:T(8,128)}, f32[2,2,256,432]{2,3,1,0:T(8,128)S(1)}, u32[]{:S(2)}, u32[]{:S(2)}) %collective-permute-start) | collective-permute-done | bytes 1769504 | tf_op jit(solution)/shard_map/while/body/eval_jaxpr/ppermute | solution.py:17
  518.8 5.3 collective-permute-start
  524.1 35.1 %collective-permute-done = f32[2,2,256,432]{2,3,1,0:T(8,128)S(1)} collective-permute-done((f32[2,2,256,432]{2,3,1,0:T(8,128)}, f32[2,2,256,432]{2,3,1,0:T(8,128)S(1)}, u32[]{:S(2)}, u32[]{:S(2)}) %collective-permute-start) | collective-permute-done | bytes 1769504 | tf_op jit(solution)/shard_map/while/body/eval_jaxpr/ppermute | solution.py:17
  559.7 3.5 bitcast_reduce_fusion
  566.3 6.9 multiply_convert_fusion.6
  573.2 6.7 fusion.64
  582.2 19.7 all-gather.1
  601.9 65.3 %all-reduce.8.cloned.1.call-done = f32[512,2048]{1,0:T(8,128)} async-done(((f32[512,2048]{1,0:T(8,128)}), f32[512,2048]{1,0:T(8,128)}) %all-reduce.8.cloned.1.call-update) | async-done | bytes 4194320 | tf_op jit(solution)/shard_map/psum | solution.py:251
  674.6 62.0 %all-gather.21.cloned.1.call-done = bf16[2048,864]{0,1:T(8,128)(2,1)} async-done(((bf16[256,864]{0,1:T(8,128)(2,1)}), bf16[2048,864]{0,1:T(8,128)(2,1)}) %all-gather.21.cloned.1.call-update) | async-done | bytes 3538960 | tf_op jit(solution)/shard_map/all_gather | solution.py:199
  736.6 5.9 fusion.65
  742.5 61.6 %all-gather.23.cloned.1.call-done = bf16[2048,864]{0,1:T(8,128)(2,1)} async-done(((bf16[256,864]{0,1:T(8,128)(2,1)}), bf16[2048,864]{0,1:T(8,128)(2,1)}) %all-gather.23.cloned.1.call-update) | async-done | bytes 3538960 | tf_op jit(solution)/shard_map/all_gather | solution.py:200
  804.0 5.9 fusion.66
  809.9 61.5 %all-gather.25.cloned.1.call-done = bf16[864,2048]{1,0:T(8,128)(2,1)} async-done(((bf16[864,256]{1,0:T(8,128)(2,1)}), bf16[864,2048]{1,0:T(8,128)(2,1)}) %all-gather.25.cloned.1.call-update) | async-done | bytes 3538960 | tf_op jit(solution)/shard_map/all_gather | solution.py:201
  871.5 7.4 multiply_convert_fusion.3
  881.5 4.5 convolution_add_fusion
  886.5 6.6 fusion.67
  893.1 76.8 %all-reduce.10.cloned.1.call-done = f32[512,2048]{1,0:T(8,128)} async-done(((f32[512,2048]{1,0:T(8,128)}), f32[512,2048]{1,0:T(8,128)}) %all-reduce.10.cloned.1.call-update) | async-done | bytes 4194320 | tf_op jit(solution)/shard_map/psum | solution.py:293
  969.9 5.3 multiply_reduce_fusion
  979.5 4.2 fusion.55
  1001.3 293.0 %while.21 = (s32[]{:T(128)}, f32[2,2,256,432]{2,3,1,0:T(8,128)S(1)}, f32[2]{0:T(128)S(1)}, f32[2,2,256,432]{2,3,1,0:T(8,128)S(1)}, s32[]{:T(128)}) while((s32[]{:T(128)}, f32[2,2,256,432]{2,3,1,0:T(8,128)S(1)}, f32[2]{0:T(128)S(1)}, f32[2,2,256,432]{2,3,1,0:T(8,128)S(1)}, s32[]{:T(128)}) %tuple.110), condition=%wide.region_16.17_spmd, body=%wide.region_15.16_spmd.sunk | while | flops 884738 | bytes 12386413 | solution.py:172
  1004.1 40.8 %collective-permute-done.1 = f32[2,2,256,432]{2,3,1,0:T(8,128)S(1)} collective-permute-done((f32[2,2,256,432]{2,3,1,0:T(8,128)}, f32[2,2,256,432]{2,3,1,0:T(8,128)S(1)}, u32[]{:S(2)}, u32[]{:S(2)}) %collective-permute-start.1) | collective-permute-done | bytes 1769504 | tf_op jit(solution)/shard_map/while/body/eval_jaxpr/ppermute | solution.py:17
  1047.8 40.6 %collective-permute-done.1 = f32[2,2,256,432]{2,3,1,0:T(8,128)S(1)} collective-permute-done((f32[2,2,256,432]{2,3,1,0:T(8,128)}, f32[2,2,256,432]{2,3,1,0:T(8,128)S(1)}, u32[]{:S(2)}, u32[]{:S(2)}) %collective-permute-start.1) | collective-permute-done | bytes 1769504 | tf_op jit(solution)/shard_map/while/body/eval_jaxpr/ppermute | solution.py:17
  1091.2 40.0 %collective-permute-done.1 = f32[2,2,256,432]{2,3,1,0:T(8,128)S(1)} collective-permute-done((f32[2,2,256,432]{2,3,1,0:T(8,128)}, f32[2,2,256,432]{2,3,1,0:T(8,128)S(1)}, u32[]{:S(2)}, u32[]{:S(2)}) %collective-permute-start.1) | collective-permute-done | bytes 1769504 | tf_op jit(solution)/shard_map/while/body/eval_jaxpr/ppermute | solution.py:17
  1134.1 39.2 %collective-permute-done.1 = f32[2,2,256,432]{2,3,1,0:T(8,128)S(1)} collective-permute-done((f32[2,2,256,432]{2,3,1,0:T(8,128)}, f32[2,2,256,432]{2,3,1,0:T(8,128)S(1)}, u32[]{:S(2)}, u32[]{:S(2)}) %collective-permute-start.1) | collective-permute-done | bytes 1769504 | tf_op jit(solution)/shard_map/while/body/eval_jaxpr/ppermute | solution.py:17
  1176.1 38.3 %collective-permute-done.1 = f32[2,2,256,432]{2,3,1,0:T(8,128)S(1)} collective-permute-done((f32[2,2,256,432]{2,3,1,0:T(8,128)}, f32[2,2,256,432]{2,3,1,0:T(8,128)S(1)}, u32[]{:S(2)}, u32[]{:S(2)}) %collective-permute-start.1) | collective-permute-done | bytes 1769504 | tf_op jit(solution)/shard_map/while/body/eval_jaxpr/ppermute | solution.py:17
  1217.2 37.5 %collective-permute-done.1 = f32[2,2,256,432]{2,3,1,0:T(8,128)S(1)} collective-permute-done((f32[2,2,256,432]{2,3,1,0:T(8,128)}, f32[2,2,256,432]{2,3,1,0:T(8,128)S(1)}, u32[]{:S(2)}, u32[]{:S(2)}) %collective-permute-start.1) | collective-permute-done | bytes 1769504 | tf_op jit(solution)/shard_map/while/body/eval_jaxpr/ppermute | solution.py:17
  1257.5 36.6 %collective-permute-done.1 = f32[2,2,256,432]{2,3,1,0:T(8,128)S(1)} collective-permute-done((f32[2,2,256,432]{2,3,1,0:T(8,128)}, f32[2,2,256,432]{2,3,1,0:T(8,128)S(1)}, u32[]{:S(2)}, u32[]{:S(2)}) %collective-permute-start.1) | collective-permute-done | bytes 1769504 | tf_op jit(solution)/shard_map/while/body/eval_jaxpr/ppermute | solution.py:17
  1294.3 3.8 broadcast_multiply_fusion
  1328.2 6.4 fusion.78
  1335.7 6.6 fusion.79
  1343.5 6.6 fusion.75
  1351.2 7.1 fusion.44
  1359.4 4.9 fusion.76
  1366.2 4.9 fusion.77
  1373.0 101.1 %all-reduce.12.cloned.1.call-done = (f32[512,2048]{1,0:T(8,128)}, f32[512,2048]{1,0:T(8,128)}) async-done(((f32[512,2048]{1,0:T(8,128)}, f32[512,2048]{1,0:T(8,128)}), (f32[512,2048]{1,0:T(8,128)}, f32[512,2048]{1,0:T(8,128)})) %all-reduce.12.cloned.1.call-update) | async-done | bytes 8388624 | tf_op jit(solution)/shard_map/psum | solution.py:259
  1477.6 38.5 %all-reduce.2 = (f32[2048]{0:T(1024)S(1)}, f32[2048]{0:T(1024)S(1)}) all-reduce(f32[2048]{0:T(1024)S(1)} %get-tuple-element.76, f32[2048]{0:T(1024)S(1)} %copy-done.58), channel_id=2, replica_groups=mesh['seq'=8,'tp'=4] {'seq'}, use_global_device_ids=true, to_apply=%region_21.22.clone | all-reduce | flops 4096 | bytes 32768
  1517.3 5.6 add_convert_fusion
  1527.2 39.8 %reduce-scatter.11.cloned.1.call-done = f32[256,512]{1,0:T(8,128)} async-done(((f32[2048,512]{1,0:T(8,128)}), f32[256,512]{1,0:T(8,128)}) %reduce-scatter.11.cloned.1.call-update) | async-done | bytes 524304 | tf_op jit(solution)/shard_map/reduce_scatter | solution.py:354
  1567.0 92.2 %reduce-scatter.9.cloned.1.call-done = f32[256,512]{1,0:T(8,128)} async-done(((f32[2048,512]{1,0:T(8,128)}), f32[256,512]{1,0:T(8,128)}) %reduce-scatter.9.cloned.1.call-update) | async-done | bytes 524304 | tf_op jit(solution)/shard_map/reduce_scatter | solution.py:353
  1659.2 133.3 %reduce-scatter.19.cloned.1.call-done = f32[256,864]{0,1:T(8,128)} async-done(((f32[2048,864]{0,1:T(8,128)}), f32[256,864]{0,1:T(8,128)}) %reduce-scatter.19.cloned.1.call-update) | async-done | bytes 884752 | tf_op jit(solution)/shard_map/reduce_scatter | solution.py:358
  1792.5 132.8 %reduce-scatter.21.cloned.1.call-done = f32[256,864]{0,1:T(8,128)} async-done(((f32[2048,864]{0,1:T(8,128)}), f32[256,864]{0,1:T(8,128)}) %reduce-scatter.21.cloned.1.call-update) | async-done | bytes 884752 | tf_op jit(solution)/shard_map/reduce_scatter | solution.py:359
  1925.3 132.8 %reduce-scatter.23.cloned.1.call-done = f32[864,256]{1,0:T(8,128)} async-done(((f32[864,2048]{1,0:T(8,128)}), f32[864,256]{1,0:T(8,128)}) %reduce-scatter.23.cloned.1.call-update) | async-done | bytes 884752 | tf_op jit(solution)/shard_map/reduce_scatter | solution.py:360
  2058.2 132.8 %reduce-scatter.17.cloned.1.call-done = f32[864,256]{1,0:T(8,128)} async-done(((f32[864,2048]{1,0:T(8,128)}), f32[864,256]{1,0:T(8,128)}) %reduce-scatter.17.cloned.1.call-update) | async-done | bytes 884752 | tf_op jit(solution)/shard_map/reduce_scatter | solution.py:357
  2191.0 132.8 %reduce-scatter.13.cloned.1.call-done = f32[256,864]{0,1:T(8,128)} async-done(((f32[2048,864]{0,1:T(8,128)}), f32[256,864]{0,1:T(8,128)}) %reduce-scatter.13.cloned.1.call-update) | async-done | bytes 884752 | tf_op jit(solution)/shard_map/reduce_scatter | solution.py:355
  2323.8 133.0 %reduce-scatter.15.cloned.1.call-done = f32[256,864]{0,1:T(8,128)} async-done(((f32[2048,864]{0,1:T(8,128)}), f32[256,864]{0,1:T(8,128)}) %reduce-scatter.15.cloned.1.call-update) | async-done | bytes 884752 | tf_op jit(solution)/shard_map/reduce_scatter | solution.py:356
  (279 shorter events, 133.4 us)
Async XLA Ops:
  7.2 3.6 copy-start.63
  7.2 26.1 %copy-start.2 = (bf16[2,256,2048]{2,1,0:T(8,128)(2,1)S(1)}, bf16[2,256,2048]{2,1,0:T(8,128)(2,1)}, u32[]{:S(2)}) copy-start(bf16[2,256,2048]{2,1,0:T(8,128)(2,1)} %param.17) | copy-start | bytes 6291460
  7.2 54.9 %all-gather.17.cloned.1.call-start = ((), (), s32[]{:S(2)}) async-start(), calls=%async_computation.11 | async-start | bytes 2359296 | tf_op jit(solution)/shard_map/all_gather | solution.py:195
  7.9 103.9 %all-gather.15.cloned.1.call-start = ((), (), s32[]{:S(2)}) async-start(), calls=%async_computation.10 | async-start | bytes 2359296 | tf_op jit(solution)/shard_map/all_gather | solution.py:194
  8.7 171.0 %all-gather.13.cloned.1.call-start = ((), (), s32[]{:S(2)}) async-start(), calls=%async_computation.9 | async-start | bytes 3981312 | tf_op jit(solution)/shard_map/all_gather | solution.py:196
  9.4 556.9 %all-gather.11.cloned.1.call-start = ((), (), s32[]{:S(2)}) async-start(), calls=%async_computation.8 | async-start | bytes 3981312 | tf_op jit(solution)/shard_map/all_gather | solution.py:197
  10.0 563.2 %all-gather.19.cloned.1.call-start = ((), (), s32[]{:S(2)}) async-start(), calls=%async_computation.12 | async-start | bytes 3981312 | tf_op jit(solution)/shard_map/all_gather | solution.py:198
  10.6 656.7 %all-reduce.8.cloned.1.call-start = ((), (), s32[]{:S(2)}) async-start(), calls=%async_computation.13 | async-start | bytes 8388608 | tf_op jit(solution)/shard_map/psum | solution.py:251
  33.3 4.0 copy-start.46
  34.9 85.6 %copy-start.39 = (f32[256,256]{0,1:T(8,128)}, f32[256,256]{0,1:T(8,128)S(1)}, u32[]{:S(2)}) copy-start(f32[256,256]{0,1:T(8,128)S(1)} %pad_maximum_fusion) | copy-start | bytes 786436
  35.0 85.6 %copy-start.38 = (f32[256,256]{0,1:T(8,128)}, f32[256,256]{0,1:T(8,128)S(1)}, u32[]{:S(2)}) copy-start(f32[256,256]{0,1:T(8,128)S(1)} %pad_maximum_fusion.1) | copy-start | bytes 786436
  37.2 83.8 %copy-start.30 = (f32[2,256,256]{2,1,0:T(8,128)}, f32[2,256,256]{2,1,0:T(8,128)S(1)}, u32[]{:S(2)}) copy-start(f32[2,256,256]{2,1,0:T(8,128)S(1)} %exponential_select_fusion) | copy-start | bytes 1572868
  37.3 148.1 %copy-start.59 = (f32[256,2]{0,1:T(2,128)}, f32[256,2]{0,1:T(2,128)S(1)}, u32[]{:S(2)}) copy-start(f32[256,2]{0,1:T(2,128)S(1)} %get-tuple-element.128) | copy-start | bytes 6148
  37.3 522.4 %copy-start.61 = (f32[256,2]{0,1:T(2,128)}, f32[256,2]{0,1:T(2,128)S(1)}, u32[]{:S(2)}) copy-start(f32[256,2]{0,1:T(2,128)S(1)} %get-tuple-element.127) | copy-start | bytes 6148
  111.9 4.1 copy-start.6
  116.0 3.0 copy-start.42
  122.3 61.4 %copy-start.28 = (bf16[2,2,256,256]{3,2,1,0:T(8,128)(2,1)}, bf16[2,2,256,256]{3,2,1,0:T(8,128)(2,1)S(1)}, u32[]{:S(2)}) copy-start(bf16[2,2,256,256]{3,2,1,0:T(8,128)(2,1)S(1)} %fusion.35) | copy-start | bytes 1572868
  188.2 52.4 %collective-permute-start = (f32[2,2,256,432]{2,3,1,0:T(8,128)}, f32[2,2,256,432]{2,3,1,0:T(8,128)S(1)}, u32[]{:S(2)}, u32[]{:S(2)}) collective-permute-start(f32[2,2,256,432]{2,3,1,0:T(8,128)} %multiply_add_fusion.5), channel_id=1, source_target_pairs={{0,4},{4,8},{8,12},{12,16},{16,20},{20,24},{24,28},{1,5},{5,9},{9,... | collective-permute-start | bytes 5308424 | tf_op jit(solution)/shard_map/while/body/eval_jaxpr/ppermute | solution.py:17
  242.2 65.5 %collective-permute-start = (f32[2,2,256,432]{2,3,1,0:T(8,128)}, f32[2,2,256,432]{2,3,1,0:T(8,128)S(1)}, u32[]{:S(2)}, u32[]{:S(2)}) collective-permute-start(f32[2,2,256,432]{2,3,1,0:T(8,128)} %multiply_add_fusion.5), channel_id=1, source_target_pairs={{0,4},{4,8},{8,12},{12,16},{16,20},{20,24},{24,28},{1,5},{5,9},{9,... | collective-permute-start | bytes 5308424 | tf_op jit(solution)/shard_map/while/body/eval_jaxpr/ppermute | solution.py:17
  309.3 68.5 %collective-permute-start = (f32[2,2,256,432]{2,3,1,0:T(8,128)}, f32[2,2,256,432]{2,3,1,0:T(8,128)S(1)}, u32[]{:S(2)}, u32[]{:S(2)}) collective-permute-start(f32[2,2,256,432]{2,3,1,0:T(8,128)} %multiply_add_fusion.5), channel_id=1, source_target_pairs={{0,4},{4,8},{8,12},{12,16},{16,20},{20,24},{24,28},{1,5},{5,9},{9,... | collective-permute-start | bytes 5308424 | tf_op jit(solution)/shard_map/while/body/eval_jaxpr/ppermute | solution.py:17
  379.3 51.4 %collective-permute-start = (f32[2,2,256,432]{2,3,1,0:T(8,128)}, f32[2,2,256,432]{2,3,1,0:T(8,128)S(1)}, u32[]{:S(2)}, u32[]{:S(2)}) collective-permute-start(f32[2,2,256,432]{2,3,1,0:T(8,128)} %multiply_add_fusion.5), channel_id=1, source_target_pairs={{0,4},{4,8},{8,12},{12,16},{16,20},{20,24},{24,28},{1,5},{5,9},{9,... | collective-permute-start | bytes 5308424 | tf_op jit(solution)/shard_map/while/body/eval_jaxpr/ppermute | solution.py:17
  432.3 42.1 %collective-permute-start = (f32[2,2,256,432]{2,3,1,0:T(8,128)}, f32[2,2,256,432]{2,3,1,0:T(8,128)S(1)}, u32[]{:S(2)}, u32[]{:S(2)}) collective-permute-start(f32[2,2,256,432]{2,3,1,0:T(8,128)} %multiply_add_fusion.5), channel_id=1, source_target_pairs={{0,4},{4,8},{8,12},{12,16},{16,20},{20,24},{24,28},{1,5},{5,9},{9,... | collective-permute-start | bytes 5308424 | tf_op jit(solution)/shard_map/while/body/eval_jaxpr/ppermute | solution.py:17
  476.0 41.2 %collective-permute-start = (f32[2,2,256,432]{2,3,1,0:T(8,128)}, f32[2,2,256,432]{2,3,1,0:T(8,128)S(1)}, u32[]{:S(2)}, u32[]{:S(2)}) collective-permute-start(f32[2,2,256,432]{2,3,1,0:T(8,128)} %multiply_add_fusion.5), channel_id=1, source_target_pairs={{0,4},{4,8},{8,12},{12,16},{16,20},{20,24},{24,28},{1,5},{5,9},{9,... | collective-permute-start | bytes 5308424 | tf_op jit(solution)/shard_map/while/body/eval_jaxpr/ppermute | solution.py:17
  518.8 40.4 %collective-permute-start = (f32[2,2,256,432]{2,3,1,0:T(8,128)}, f32[2,2,256,432]{2,3,1,0:T(8,128)S(1)}, u32[]{:S(2)}, u32[]{:S(2)}) collective-permute-start(f32[2,2,256,432]{2,3,1,0:T(8,128)} %multiply_add_fusion.5), channel_id=1, source_target_pairs={{0,4},{4,8},{8,12},{12,16},{16,20},{20,24},{24,28},{1,5},{5,9},{9,... | collective-permute-start | bytes 5308424 | tf_op jit(solution)/shard_map/while/body/eval_jaxpr/ppermute | solution.py:17
  559.7 3.5 copy-start.50
  579.9 156.7 %all-gather.21.cloned.1.call-start = ((), (), s32[]{:S(2)}) async-start(), calls=%async_computation.14 | async-start | bytes 3981312 | tf_op jit(solution)/shard_map/all_gather | solution.py:199
  580.6 223.4 %all-gather.23.cloned.1.call-start = ((), (), s32[]{:S(2)}) async-start(), calls=%async_computation.15 | async-start | bytes 3981312 | tf_op jit(solution)/shard_map/all_gather | solution.py:200
  581.4 290.1 %all-gather.25.cloned.1.call-start = ((), (), s32[]{:S(2)}) async-start(), calls=%async_computation.16 | async-start | bytes 3981312 | tf_op jit(solution)/shard_map/all_gather | solution.py:201
  582.1 387.7 %all-reduce.10.cloned.1.call-start = ((), (), s32[]{:S(2)}) async-start(), calls=%async_computation.17 | async-start | bytes 8388608 | tf_op jit(solution)/shard_map/psum | solution.py:293
  871.5 7.4 copy-start.21
  886.0 588.0 %all-reduce.12.cloned.1.call-start = ((), (), s32[]{:S(2)}) async-start(), calls=%async_computation.26 | async-start | bytes 16777216 | tf_op jit(solution)/shard_map/psum | solution.py:259
  969.9 5.3 copy-start.1
  969.9 5.9 copy-start.8
  969.9 5.9 copy-start.49
  969.9 6.0 copy-start.57
  975.8 3.4 copy-start.20
  975.8 3.4 copy-start.43
  975.8 3.7 copy-start.67
  979.2 4.5 copy-start.4
  998.1 3.1 copy-start.51
  1001.3 293.0 %copy-start.60 = (f32[256,2]{0,1:T(2,128)S(1)}, f32[256,2]{0,1:T(2,128)}, u32[]{:S(2)}) copy-start(f32[256,2]{0,1:T(2,128)} %copy-done.59) | copy-start | bytes 6148
  1002.8 42.1 %collective-permute-start.1 = (f32[2,2,256,432]{2,3,1,0:T(8,128)}, f32[2,2,256,432]{2,3,1,0:T(8,128)S(1)}, u32[]{:S(2)}, u32[]{:S(2)}) collective-permute-start(f32[2,2,256,432]{2,3,1,0:T(8,128)} %multiply_add_fusion.6), channel_id=1, source_target_pairs={{4,0},{8,4},{12,8},{16,12},{20,16},{24,20},{28,24},{5,1},{9,5},{13... | collective-permute-start | bytes 5308424 | tf_op jit(solution)/shard_map/while/body/eval_jaxpr/ppermute | solution.py:17
  1046.5 41.9 %collective-permute-start.1 = (f32[2,2,256,432]{2,3,1,0:T(8,128)}, f32[2,2,256,432]{2,3,1,0:T(8,128)S(1)}, u32[]{:S(2)}, u32[]{:S(2)}) collective-permute-start(f32[2,2,256,432]{2,3,1,0:T(8,128)} %multiply_add_fusion.6), channel_id=1, source_target_pairs={{4,0},{8,4},{12,8},{16,12},{20,16},{24,20},{28,24},{5,1},{9,5},{13... | collective-permute-start | bytes 5308424 | tf_op jit(solution)/shard_map/while/body/eval_jaxpr/ppermute | solution.py:17
  1089.9 41.3 %collective-permute-start.1 = (f32[2,2,256,432]{2,3,1,0:T(8,128)}, f32[2,2,256,432]{2,3,1,0:T(8,128)S(1)}, u32[]{:S(2)}, u32[]{:S(2)}) collective-permute-start(f32[2,2,256,432]{2,3,1,0:T(8,128)} %multiply_add_fusion.6), channel_id=1, source_target_pairs={{4,0},{8,4},{12,8},{16,12},{20,16},{24,20},{28,24},{5,1},{9,5},{13... | collective-permute-start | bytes 5308424 | tf_op jit(solution)/shard_map/while/body/eval_jaxpr/ppermute | solution.py:17
  1132.8 40.5 %collective-permute-start.1 = (f32[2,2,256,432]{2,3,1,0:T(8,128)}, f32[2,2,256,432]{2,3,1,0:T(8,128)S(1)}, u32[]{:S(2)}, u32[]{:S(2)}) collective-permute-start(f32[2,2,256,432]{2,3,1,0:T(8,128)} %multiply_add_fusion.6), channel_id=1, source_target_pairs={{4,0},{8,4},{12,8},{16,12},{20,16},{24,20},{28,24},{5,1},{9,5},{13... | collective-permute-start | bytes 5308424 | tf_op jit(solution)/shard_map/while/body/eval_jaxpr/ppermute | solution.py:17
  1174.8 39.6 %collective-permute-start.1 = (f32[2,2,256,432]{2,3,1,0:T(8,128)}, f32[2,2,256,432]{2,3,1,0:T(8,128)S(1)}, u32[]{:S(2)}, u32[]{:S(2)}) collective-permute-start(f32[2,2,256,432]{2,3,1,0:T(8,128)} %multiply_add_fusion.6), channel_id=1, source_target_pairs={{4,0},{8,4},{12,8},{16,12},{20,16},{24,20},{28,24},{5,1},{9,5},{13... | collective-permute-start | bytes 5308424 | tf_op jit(solution)/shard_map/while/body/eval_jaxpr/ppermute | solution.py:17
  1216.0 38.7 %collective-permute-start.1 = (f32[2,2,256,432]{2,3,1,0:T(8,128)}, f32[2,2,256,432]{2,3,1,0:T(8,128)S(1)}, u32[]{:S(2)}, u32[]{:S(2)}) collective-permute-start(f32[2,2,256,432]{2,3,1,0:T(8,128)} %multiply_add_fusion.6), channel_id=1, source_target_pairs={{4,0},{8,4},{12,8},{16,12},{20,16},{24,20},{28,24},{5,1},{9,5},{13... | collective-permute-start | bytes 5308424 | tf_op jit(solution)/shard_map/while/body/eval_jaxpr/ppermute | solution.py:17
  1256.3 37.9 %collective-permute-start.1 = (f32[2,2,256,432]{2,3,1,0:T(8,128)}, f32[2,2,256,432]{2,3,1,0:T(8,128)S(1)}, u32[]{:S(2)}, u32[]{:S(2)}) collective-permute-start(f32[2,2,256,432]{2,3,1,0:T(8,128)} %multiply_add_fusion.6), channel_id=1, source_target_pairs={{4,0},{8,4},{12,8},{16,12},{20,16},{24,20},{28,24},{5,1},{9,5},{13... | collective-permute-start | bytes 5308424 | tf_op jit(solution)/shard_map/while/body/eval_jaxpr/ppermute | solution.py:17
  1300.6 3.7 copy-start.15
  1318.6 248.4 %reduce-scatter.11.cloned.1.call-start = ((), (), s32[]{:S(2)}) async-start(), calls=%async_computation.19 | async-start | bytes 4718592 | tf_op jit(solution)/shard_map/reduce_scatter | solution.py:354
  1323.5 335.7 %reduce-scatter.9.cloned.1.call-start = ((), (), s32[]{:S(2)}) async-start(), calls=%async_computation.18 | async-start | bytes 4718592 | tf_op jit(solution)/shard_map/reduce_scatter | solution.py:353
  1327.0 465.5 %reduce-scatter.19.cloned.1.call-start = ((), (), s32[]{:S(2)}) async-start(), calls=%async_computation.23 | async-start | bytes 7962624 | tf_op jit(solution)/shard_map/reduce_scatter | solution.py:358
  1334.6 590.7 %reduce-scatter.21.cloned.1.call-start = ((), (), s32[]{:S(2)}) async-start(), calls=%async_computation.24 | async-start | bytes 7962624 | tf_op jit(solution)/shard_map/reduce_scatter | solution.py:359
  1342.3 715.8 %reduce-scatter.23.cloned.1.call-start = ((), (), s32[]{:S(2)}) async-start(), calls=%async_computation.25 | async-start | bytes 7962624 | tf_op jit(solution)/shard_map/reduce_scatter | solution.py:360
  1350.1 840.9 %reduce-scatter.17.cloned.1.call-start = ((), (), s32[]{:S(2)}) async-start(), calls=%async_computation.22 | async-start | bytes 7962624 | tf_op jit(solution)/shard_map/reduce_scatter | solution.py:357
  1358.3 965.6 %reduce-scatter.13.cloned.1.call-start = ((), (), s32[]{:S(2)}) async-start(), calls=%async_computation.20 | async-start | bytes 7962624 | tf_op jit(solution)/shard_map/reduce_scatter | solution.py:355
  1364.4 1092.5 %reduce-scatter.15.cloned.1.call-start = ((), (), s32[]{:S(2)}) async-start(), calls=%async_computation.21 | async-start | bytes 7962624 | tf_op jit(solution)/shard_map/reduce_scatter | solution.py:356
  1371.1 102.9 %copy-start.3 = (bf16[2,256,2048]{2,1,0:T(8,128)(2,1)S(1)}, bf16[2,256,2048]{2,1,0:T(8,128)(2,1)}, u32[]{:S(2)}) copy-start(bf16[2,256,2048]{2,1,0:T(8,128)(2,1)} %param.17) | copy-start | bytes 6291460
  1371.1 102.9 %copy-start.47 = (f32[8,1,256]{2,1,0:T(1,128)S(1)}, f32[8,1,256]{2,1,0:T(1,128)}, u32[]{:S(2)}) copy-start(f32[8,1,256]{2,1,0:T(1,128)} %copy-done.46) | copy-start | bytes 24580
  1371.1 102.9 %copy-start.53 = (f32[1,2,2,128]{3,1,2,0:T(2,128)S(1)}, f32[1,2,2,128]{3,1,2,0:T(2,128)}, u32[]{:S(2)}) copy-start(f32[1,2,2,128]{3,1,2,0:T(2,128)} %copy-done.52) | copy-start | bytes 6148
  1371.1 102.9 %copy-start.55 = (f32[1,2,2,128]{3,1,2,0:T(2,128)S(1)}, f32[1,2,2,128]{3,1,2,0:T(2,128)}, u32[]{:S(2)}) copy-start(f32[1,2,2,128]{3,1,2,0:T(2,128)} %copy-done.54) | copy-start | bytes 6148
  1474.1 3.5 copy-start.58
  1517.3 5.7 copy-start.5
  1517.3 6.9 copy-start.9
  (37 other events, 63.7 us)
Sparse Core Ops, SparseCore 0:
  10.1 51.9 all-gather.16
  64.2 47.6 all-gather.14
  113.9 65.6 all-gather.12
  181.6 92.4 all-gather.10
  276.0 88.9 all-gather.18
  580.0 87.2 all-reduce.7
  669.3 67.2 all-gather.20
  738.7 65.3 all-gather.22
  806.1 65.3 all-gather.24
  886.2 83.6 all-reduce.9
  1318.7 155.3 all-reduce.11
  1478.1 88.8 reduce-scatter.10
  1571.2 87.9 reduce-scatter.8
  1663.3 129.1 reduce-scatter.18
  1796.6 128.6 reduce-scatter.20
  1929.5 128.6 reduce-scatter.22
  2062.3 128.6 reduce-scatter.16
  2195.1 128.6 reduce-scatter.12
  2328.1 128.6 reduce-scatter.14
where the time goes:
time: 2470 us; the launch traced here: 2460 us
  waiting for transfers between devices  2050 us (83%)
  matrix products  132 us (5%)
  starting transfers between devices  85.1 us (3%)
  blocking collectives  80.6 us (3%)
  other arithmetic  62.5 us (3%)
  local copies, waits for them, and re-layouts  37.7 us (2%)
    ppermute x14, waiting for transfers between devices, passed_along(): return lax.ppermute(block, axis, route)  560 us
    reduce_scatter x1, waiting for transfers between devices, on_device(): lax.psum_scatter(glu_grad, 'seq', scatter_dimension=0, tiled=True)  133 us
    reduce_scatter x1, waiting for transfers between devices, on_device(): lax.psum_scatter(gate_grad, 'seq', scatter_dimension=0, tiled=True)  133 us
    reduce_scatter x1, waiting for transfers between devices, on_device(): lax.psum_scatter(value_grad, 'seq', scatter_dimension=0, tiled=True)  133 us
    reduce_scatter x1, waiting for transfers between devices, on_device(): lax.psum_scatter(down_grad, 'seq', scatter_dimension=1, tiled=True)  133 us
    reduce_scatter x1, waiting for transfers between devices, on_device(): lax.psum_scatter(out_grad, 'seq', scatter_dimension=1, tiled=True)  133 us
    reduce_scatter x1, waiting for transfers between devices, on_device(): lax.psum_scatter(up_grad, 'seq', scatter_dimension=0, tiled=True)  133 us
    psum x1, waiting for transfers between devices, on_device(): lax.psum(jnp.dot(hidden, full_down, preferred_element_type=jnp.float32),...  101 us
  transfers between devices with their start and end apart: 33, of which 31 were waited for; matrix products, arithmetic and copies ran while one was open for 5% of the time, Pallas kernels for 0%

commit v1 on v0

--- a/solution.py
+++ b/solution.py
@@ -9,6 +9,18 @@
 EPS_LAYER = 1e-05
 EPS_GROUP = 1e-06
 MAXIMAL_ACCURACY = lax.Precision.HIGHEST
+
+
+def doubled_up(x, axis, dim):
+    ways, here = (lax.axis_size(axis), lax.axis_index(axis))
+    grown, reach = (x, 1)
+    while reach < ways:
+        theirs = lax.ppermute(grown, axis, [(d, d ^ reach) for d in range(ways)])
+        mine_first = jnp.concatenate([grown, theirs], axis=dim)
+        theirs_first = jnp.concatenate([theirs, grown], axis=dim)
+        grown = jnp.where(here & reach == 0, mine_first, theirs_first)
+        reach = 2 * reach
+    return grown
 
 
 def passed_along(block, axis, distance):
@@ -193,7 +205,7 @@
     gathered = (
         lax.all_gather(w_query, "seq", axis=0, tiled=True),
         lax.all_gather(w_key, "seq", axis=0, tiled=True),
-        lax.all_gather(w_value, "seq", axis=0, tiled=True),
+        doubled_up(w_value, "seq", 0),
         lax.all_gather(w_gate, "seq", axis=0, tiled=True),
         lax.all_gather(w_out, "seq", axis=1, tiled=True),
         lax.all_gather(w_glu, "seq", axis=0, tiled=True),

time: 2470 us -> 2500 us (1.012)
    ppermute x0 -> x3, waiting for transfers between devices: none -> 112 us  [doubled_up(): theirs = lax.ppermute(grown, axis, [(d, d ^ reach) for d in range(ways)])]
    all_gather x1, waiting for transfers between devices: 57.4 us -> 0.01 us  [on_device(): lax.all_gather(w_value, 'seq', axis=0, tiled=True)]
    all_gather x1, waiting for transfers between devices: 45.9 us -> 13.8 us  [on_device(): lax.all_gather(w_query, 'seq', axis=0, tiled=True)]
  transfers between devices with their start and end apart: 33 -> 36, of which waited for: 31 -> 31; matrix products, arithmetic and copies ran while one was open for 5% -> 8% of each run, Pallas kernels for 0% -> 0%
where the time goes in v1:
time: 2500 us
  waiting for transfers between devices  2060 us (82%)
  matrix products  138 us (6%)
  starting transfers between devices  91.9 us (4%)
  blocking collectives  85.4 us (3%)
  other arithmetic  65.4 us (3%)
  local copies, waits for them, and re-layouts  41.3 us (2%)
    ppermute x14, waiting for transfers between devices, passed_along(): return lax.ppermute(block, axis, route)  574 us
    reduce_scatter x1, waiting for transfers between devices, on_device(): lax.psum_scatter(glu_grad, 'seq', scatter_dimension=0, tiled=True)  133 us
    reduce_scatter x1, waiting for transfers between devices, on_device(): lax.psum_scatter(gate_grad, 'seq', scatter_dimension=0, tiled=True)  133 us
    reduce_scatter x1, waiting for transfers between devices, on_device(): lax.psum_scatter(out_grad, 'seq', scatter_dimension=1, tiled=True)  133 us
    reduce_scatter x1, waiting for transfers between devices, on_device(): lax.psum_scatter(value_grad, 'seq', scatter_dimension=0, tiled=True)  133 us
    reduce_scatter x1, waiting for transfers between devices, on_device(): lax.psum_scatter(down_grad, 'seq', scatter_dimension=1, tiled=True)  133 us
    reduce_scatter x1, waiting for transfers between devices, on_device(): lax.psum_scatter(up_grad, 'seq', scatter_dimension=0, tiled=True)  133 us
    ppermute x3, waiting for transfers between devices, doubled_up(): theirs = lax.ppermute(grown, axis, [(d, d ^ reach) for d in range(ways)])  112 us
  transfers between devices with their start and end apart: 36, of which 31 were waited for; matrix products, arithmetic and copies ran while one was open for 8% of the time, Pallas kernels for 0%

profile of v1, /device:TPU:0, one launch (start us, length us, event | category | flops | bytes accessed | tf_op | source)
XLA Modules:
  0.0 2497.9 jit_solution(6314869416019960635)
XLA Ops:
  13.2 25.5 %all-gather = bf16[8,1,256]{2,1,0:T(2,128)(2,1)S(1)} all-gather(bf16[1,1,256]{2,1,0:T(2,128)(2,1)S(1)} %reshape.349), channel_id=1, replica_groups=mesh['seq'=8,'tp'=4] {'seq'}, dimensions={0}, use_global_device_ids=true | all-gather | bytes 4608 | tf_op jit(solution)/shard_map/all_gather | solution.py:214
  43.4 31.6 %collective-permute-done.3 = bf16[512,864]{0,1:T(8,128)(2,1)S(1)} collective-permute-done((bf16[512,864]{0,1:T(8,128)(2,1)S(1)}, bf16[512,864]{0,1:T(8,128)(2,1)S(1)}, u32[]{:S(2)}, u32[]{:S(2)}) %collective-permute-start.3) | collective-permute-done | bytes 884768 | tf_op jit(solution)/shard_map/ppermute | solution.py:18
  78.7 80.1 %collective-permute-done.4 = bf16[1024,864]{0,1:T(8,128)(2,1)S(1)} collective-permute-done((bf16[1024,864]{0,1:T(8,128)(2,1)S(1)}, bf16[1024,864]{0,1:T(8,128)(2,1)S(1)}, u32[]{:S(2)}, u32[]{:S(2)}) %collective-permute-start.4) | collective-permute-done | bytes 1769504 | tf_op jit(solution)/shard_map/ppermute | solution.py:18
  162.6 4.2 copy.81
  166.8 3.9 fusion.16
  170.7 13.8 all-gather.13.cloned.1.call-done
  184.4 3.9 copy.80
  197.2 358.0 %while.20 = (s32[]{:T(128)}, f32[2,2,256,432]{2,3,1,0:T(8,128)S(1)}, f32[2]{0:T(128)S(1)}, f32[2,2,256,432]{2,3,1,0:T(8,128)S(1)}, s32[]{:T(128)}) while((s32[]{:T(128)}, f32[2,2,256,432]{2,3,1,0:T(8,128)S(1)}, f32[2]{0:T(128)S(1)}, f32[2,2,256,432]{2,3,1,0:T(8,128)S(1)}, s32[]{:T(128)}) %tuple.66), condition=%wide.region_3.4_spmd, body=%wide.region_2.3_spmd.sunk | while | flops 884738 | bytes 12386413 | solution.py:176
  201.3 52.9 %collective-permute-done = f32[2,2,256,432]{2,3,1,0:T(8,128)S(1)} collective-permute-done((f32[2,2,256,432]{2,3,1,0:T(8,128)}, f32[2,2,256,432]{2,3,1,0:T(8,128)S(1)}, u32[]{:S(2)}, u32[]{:S(2)}) %collective-permute-start) | collective-permute-done | bytes 1769504 | tf_op jit(solution)/shard_map/while/body/eval_jaxpr/ppermute | solution.py:29
  255.7 21.2 collective-permute-start
  276.9 40.6 %collective-permute-done = f32[2,2,256,432]{2,3,1,0:T(8,128)S(1)} collective-permute-done((f32[2,2,256,432]{2,3,1,0:T(8,128)}, f32[2,2,256,432]{2,3,1,0:T(8,128)S(1)}, u32[]{:S(2)}, u32[]{:S(2)}) %collective-permute-start) | collective-permute-done | bytes 1769504 | tf_op jit(solution)/shard_map/while/body/eval_jaxpr/ppermute | solution.py:29
  319.1 22.1 collective-permute-start
  341.1 41.1 %collective-permute-done = f32[2,2,256,432]{2,3,1,0:T(8,128)S(1)} collective-permute-done((f32[2,2,256,432]{2,3,1,0:T(8,128)}, f32[2,2,256,432]{2,3,1,0:T(8,128)S(1)}, u32[]{:S(2)}, u32[]{:S(2)}) %collective-permute-start) | collective-permute-done | bytes 1769504 | tf_op jit(solution)/shard_map/while/body/eval_jaxpr/ppermute | solution.py:29
  383.8 16.4 collective-permute-start
  400.2 34.8 %collective-permute-done = f32[2,2,256,432]{2,3,1,0:T(8,128)S(1)} collective-permute-done((f32[2,2,256,432]{2,3,1,0:T(8,128)}, f32[2,2,256,432]{2,3,1,0:T(8,128)S(1)}, u32[]{:S(2)}, u32[]{:S(2)}) %collective-permute-start) | collective-permute-done | bytes 1769504 | tf_op jit(solution)/shard_map/while/body/eval_jaxpr/ppermute | solution.py:29
  436.5 5.3 collective-permute-start
  441.8 33.9 %collective-permute-done = f32[2,2,256,432]{2,3,1,0:T(8,128)S(1)} collective-permute-done((f32[2,2,256,432]{2,3,1,0:T(8,128)}, f32[2,2,256,432]{2,3,1,0:T(8,128)S(1)}, u32[]{:S(2)}, u32[]{:S(2)}) %collective-permute-start) | collective-permute-done | bytes 1769504 | tf_op jit(solution)/shard_map/while/body/eval_jaxpr/ppermute | solution.py:29
  477.3 5.3 collective-permute-start
  482.6 33.1 %collective-permute-done = f32[2,2,256,432]{2,3,1,0:T(8,128)S(1)} collective-permute-done((f32[2,2,256,432]{2,3,1,0:T(8,128)}, f32[2,2,256,432]{2,3,1,0:T(8,128)S(1)}, u32[]{:S(2)}, u32[]{:S(2)}) %collective-permute-start) | collective-permute-done | bytes 1769504 | tf_op jit(solution)/shard_map/while/body/eval_jaxpr/ppermute | solution.py:29
  517.2 5.3 collective-permute-start
  522.5 32.2 %collective-permute-done = f32[2,2,256,432]{2,3,1,0:T(8,128)S(1)} collective-permute-done((f32[2,2,256,432]{2,3,1,0:T(8,128)}, f32[2,2,256,432]{2,3,1,0:T(8,128)S(1)}, u32[]{:S(2)}, u32[]{:S(2)}) %collective-permute-start) | collective-permute-done | bytes 1769504 | tf_op jit(solution)/shard_map/while/body/eval_jaxpr/ppermute | solution.py:29
  561.9 6.9 multiply_convert_fusion.6
  568.7 6.7 fusion.64
  577.5 21.5 all-gather.1
  599.0 65.1 %all-reduce.8.cloned.1.call-done = f32[512,2048]{1,0:T(8,128)} async-done(((f32[512,2048]{1,0:T(8,128)}), f32[512,2048]{1,0:T(8,128)}) %all-reduce.8.cloned.1.call-update) | async-done | bytes 4194320 | tf_op jit(solution)/shard_map/psum | solution.py:263
  671.5 61.9 %all-gather.19.cloned.1.call-done = bf16[2048,864]{0,1:T(8,128)(2,1)} async-done(((bf16[256,864]{0,1:T(8,128)(2,1)}), bf16[2048,864]{0,1:T(8,128)(2,1)}) %all-gather.19.cloned.1.call-update) | async-done | bytes 3538960 | tf_op jit(solution)/shard_map/all_gather | solution.py:211
  733.4 5.9 fusion.65
  739.2 61.5 %all-gather.21.cloned.1.call-done = bf16[2048,864]{0,1:T(8,128)(2,1)} async-done(((bf16[256,864]{0,1:T(8,128)(2,1)}), bf16[2048,864]{0,1:T(8,128)(2,1)}) %all-gather.21.cloned.1.call-update) | async-done | bytes 3538960 | tf_op jit(solution)/shard_map/all_gather | solution.py:212
  800.8 5.9 fusion.66
  806.7 61.5 %all-gather.23.cloned.1.call-done = bf16[864,2048]{1,0:T(8,128)(2,1)} async-done(((bf16[864,256]{1,0:T(8,128)(2,1)}), bf16[864,2048]{1,0:T(8,128)(2,1)}) %all-gather.23.cloned.1.call-update) | async-done | bytes 3538960 | tf_op jit(solution)/shard_map/all_gather | solution.py:213
  868.2 7.4 multiply_convert_fusion.3
  878.2 4.5 convolution_add_fusion
  883.8 6.6 fusion.67
  890.4 76.2 %all-reduce.10.cloned.1.call-done = f32[512,2048]{1,0:T(8,128)} async-done(((f32[512,2048]{1,0:T(8,128)}), f32[512,2048]{1,0:T(8,128)}) %all-reduce.10.cloned.1.call-update) | async-done | bytes 4194320 | tf_op jit(solution)/shard_map/psum | solution.py:305
  966.6 5.2 multiply_reduce_fusion
  976.4 4.2 fusion.55
  996.8 325.5 %while.21 = (s32[]{:T(128)}, f32[2,2,256,432]{2,3,1,0:T(8,128)S(1)}, f32[2]{0:T(128)S(1)}, f32[2,2,256,432]{2,3,1,0:T(8,128)S(1)}, s32[]{:T(128)}) while((s32[]{:T(128)}, f32[2,2,256,432]{2,3,1,0:T(8,128)S(1)}, f32[2]{0:T(128)S(1)}, f32[2,2,256,432]{2,3,1,0:T(8,128)S(1)}, s32[]{:T(128)}) %tuple.111), condition=%wide.region_16.17_spmd, body=%wide.region_15.16_spmd.sunk | while | flops 884738 | bytes 12386413 | solution.py:184
  999.6 59.7 %collective-permute-done.1 = f32[2,2,256,432]{2,3,1,0:T(8,128)S(1)} collective-permute-done((f32[2,2,256,432]{2,3,1,0:T(8,128)}, f32[2,2,256,432]{2,3,1,0:T(8,128)S(1)}, u32[]{:S(2)}, u32[]{:S(2)}) %collective-permute-start.1) | collective-permute-done | bytes 1769504 | tf_op jit(solution)/shard_map/while/body/eval_jaxpr/ppermute | solution.py:29
  1062.1 50.8 %collective-permute-done.1 = f32[2,2,256,432]{2,3,1,0:T(8,128)S(1)} collective-permute-done((f32[2,2,256,432]{2,3,1,0:T(8,128)}, f32[2,2,256,432]{2,3,1,0:T(8,128)S(1)}, u32[]{:S(2)}, u32[]{:S(2)}) %collective-permute-start.1) | collective-permute-done | bytes 1769504 | tf_op jit(solution)/shard_map/while/body/eval_jaxpr/ppermute | solution.py:29
  1115.8 40.7 %collective-permute-done.1 = f32[2,2,256,432]{2,3,1,0:T(8,128)S(1)} collective-permute-done((f32[2,2,256,432]{2,3,1,0:T(8,128)}, f32[2,2,256,432]{2,3,1,0:T(8,128)S(1)}, u32[]{:S(2)}, u32[]{:S(2)}) %collective-permute-start.1) | collective-permute-done | bytes 1769504 | tf_op jit(solution)/shard_map/while/body/eval_jaxpr/ppermute | solution.py:29
  1159.3 39.9 %collective-permute-done.1 = f32[2,2,256,432]{2,3,1,0:T(8,128)S(1)} collective-permute-done((f32[2,2,256,432]{2,3,1,0:T(8,128)}, f32[2,2,256,432]{2,3,1,0:T(8,128)S(1)}, u32[]{:S(2)}, u32[]{:S(2)}) %collective-permute-start.1) | collective-permute-done | bytes 1769504 | tf_op jit(solution)/shard_map/while/body/eval_jaxpr/ppermute | solution.py:29
  1202.0 39.0 %collective-permute-done.1 = f32[2,2,256,432]{2,3,1,0:T(8,128)S(1)} collective-permute-done((f32[2,2,256,432]{2,3,1,0:T(8,128)}, f32[2,2,256,432]{2,3,1,0:T(8,128)S(1)}, u32[]{:S(2)}, u32[]{:S(2)}) %collective-permute-start.1) | collective-permute-done | bytes 1769504 | tf_op jit(solution)/shard_map/while/body/eval_jaxpr/ppermute | solution.py:29
  1243.9 38.2 %collective-permute-done.1 = f32[2,2,256,432]{2,3,1,0:T(8,128)S(1)} collective-permute-done((f32[2,2,256,432]{2,3,1,0:T(8,128)}, f32[2,2,256,432]{2,3,1,0:T(8,128)S(1)}, u32[]{:S(2)}, u32[]{:S(2)}) %collective-permute-start.1) | collective-permute-done | bytes 1769504 | tf_op jit(solution)/shard_map/while/body/eval_jaxpr/ppermute | solution.py:29
  1284.9 37.3 %collective-permute-done.1 = f32[2,2,256,432]{2,3,1,0:T(8,128)S(1)} collective-permute-done((f32[2,2,256,432]{2,3,1,0:T(8,128)}, f32[2,2,256,432]{2,3,1,0:T(8,128)S(1)}, u32[]{:S(2)}, u32[]{:S(2)}) %collective-permute-start.1) | collective-permute-done | bytes 1769504 | tf_op jit(solution)/shard_map/while/body/eval_jaxpr/ppermute | solution.py:29
  1322.4 3.8 broadcast_multiply_fusion
  1342.3 4.4 fusion.72
  1346.7 4.6 fusion.71
  1364.8 6.4 fusion.78
  1372.4 6.5 fusion.79
  1380.1 6.5 fusion.75
  1387.7 7.1 fusion.44
  1396.1 4.9 fusion.76
  1402.9 4.9 fusion.77
  1409.7 98.8 %all-reduce.12.cloned.1.call-done = (f32[512,2048]{1,0:T(8,128)}, f32[512,2048]{1,0:T(8,128)}) async-done(((f32[512,2048]{1,0:T(8,128)}, f32[512,2048]{1,0:T(8,128)}), (f32[512,2048]{1,0:T(8,128)}, f32[512,2048]{1,0:T(8,128)})) %all-reduce.12.cloned.1.call-update) | async-done | bytes 8388624 | tf_op jit(solution)/shard_map/psum | solution.py:271
  1512.0 38.5 %all-reduce.2 = (f32[2048]{0:T(1024)S(1)}, f32[2048]{0:T(1024)S(1)}) all-reduce(f32[2048]{0:T(1024)S(1)} %get-tuple-element.76, f32[2048]{0:T(1024)S(1)} %copy-done.62), channel_id=2, replica_groups=mesh['seq'=8,'tp'=4] {'seq'}, use_global_device_ids=true, to_apply=%region_21.22.clone | all-reduce | flops 4096 | bytes 32768
  1551.8 5.6 add_convert_fusion
  1561.6 39.8 %reduce-scatter.11.cloned.1.call-done = f32[256,512]{1,0:T(8,128)} async-done(((f32[2048,512]{1,0:T(8,128)}), f32[256,512]{1,0:T(8,128)}) %reduce-scatter.11.cloned.1.call-update) | async-done | bytes 524304 | tf_op jit(solution)/shard_map/reduce_scatter | solution.py:366
  1601.4 92.2 %reduce-scatter.9.cloned.1.call-done = f32[256,512]{1,0:T(8,128)} async-done(((f32[2048,512]{1,0:T(8,128)}), f32[256,512]{1,0:T(8,128)}) %reduce-scatter.9.cloned.1.call-update) | async-done | bytes 524304 | tf_op jit(solution)/shard_map/reduce_scatter | solution.py:365
  1693.6 133.3 %reduce-scatter.19.cloned.1.call-done = f32[256,864]{0,1:T(8,128)} async-done(((f32[2048,864]{0,1:T(8,128)}), f32[256,864]{0,1:T(8,128)}) %reduce-scatter.19.cloned.1.call-update) | async-done | bytes 884752 | tf_op jit(solution)/shard_map/reduce_scatter | solution.py:370
  1826.9 132.8 %reduce-scatter.21.cloned.1.call-done = f32[256,864]{0,1:T(8,128)} async-done(((f32[2048,864]{0,1:T(8,128)}), f32[256,864]{0,1:T(8,128)}) %reduce-scatter.21.cloned.1.call-update) | async-done | bytes 884752 | tf_op jit(solution)/shard_map/reduce_scatter | solution.py:371
  1959.7 132.8 %reduce-scatter.23.cloned.1.call-done = f32[864,256]{1,0:T(8,128)} async-done(((f32[864,2048]{1,0:T(8,128)}), f32[864,256]{1,0:T(8,128)}) %reduce-scatter.23.cloned.1.call-update) | async-done | bytes 884752 | tf_op jit(solution)/shard_map/reduce_scatter | solution.py:372
  2092.5 132.8 %reduce-scatter.17.cloned.1.call-done = f32[864,256]{1,0:T(8,128)} async-done(((f32[864,2048]{1,0:T(8,128)}), f32[864,256]{1,0:T(8,128)}) %reduce-scatter.17.cloned.1.call-update) | async-done | bytes 884752 | tf_op jit(solution)/shard_map/reduce_scatter | solution.py:369
  2225.4 132.8 %reduce-scatter.13.cloned.1.call-done = f32[256,864]{0,1:T(8,128)} async-done(((f32[2048,864]{0,1:T(8,128)}), f32[256,864]{0,1:T(8,128)}) %reduce-scatter.13.cloned.1.call-update) | async-done | bytes 884752 | tf_op jit(solution)/shard_map/reduce_scatter | solution.py:367
  2358.2 133.0 %reduce-scatter.15.cloned.1.call-done = f32[256,864]{0,1:T(8,128)} async-done(((f32[2048,864]{0,1:T(8,128)}), f32[256,864]{0,1:T(8,128)}) %reduce-scatter.15.cloned.1.call-update) | async-done | bytes 884752 | tf_op jit(solution)/shard_map/reduce_scatter | solution.py:368
  (293 shorter events, 145.8 us)
Async XLA Ops:
  7.2 33.6 %copy-start.2 = (bf16[2,256,2048]{2,1,0:T(8,128)(2,1)S(1)}, bf16[2,256,2048]{2,1,0:T(8,128)(2,1)}, u32[]{:S(2)}) copy-start(bf16[2,256,2048]{2,1,0:T(8,128)(2,1)} %param.17) | copy-start | bytes 6291460
  7.2 155.3 %all-gather.15.cloned.1.call-start = ((), (), s32[]{:S(2)}) async-start(), calls=%async_computation.10 | async-start | bytes 2359296 | tf_op jit(solution)/shard_map/all_gather | solution.py:207
  7.9 176.5 %all-gather.13.cloned.1.call-start = ((), (), s32[]{:S(2)}) async-start(), calls=%async_computation.9 | async-start | bytes 2359296 | tf_op jit(solution)/shard_map/all_gather | solution.py:206
  8.7 553.2 %all-gather.11.cloned.1.call-start = ((), (), s32[]{:S(2)}) async-start(), calls=%async_computation.8 | async-start | bytes 3981312 | tf_op jit(solution)/shard_map/all_gather | solution.py:209
  9.4 559.3 %all-gather.17.cloned.1.call-start = ((), (), s32[]{:S(2)}) async-start(), calls=%async_computation.11 | async-start | bytes 3981312 | tf_op jit(solution)/shard_map/all_gather | solution.py:210
  9.5 32.1 %collective-permute-start.2 = (bf16[256,864]{0,1:T(8,128)(2,1)}, bf16[256,864]{0,1:T(8,128)(2,1)S(1)}, u32[]{:S(2)}, u32[]{:S(2)}) collective-permute-start(bf16[256,864]{0,1:T(8,128)(2,1)} %param.22), channel_id=1, source_target_pairs={{0,4},{4,0},{8,12},{12,8},{16,20},{20,16},{24,28},{28,24},{1,5},{5... | collective-permute-start | bytes 1327112 | tf_op jit(solution)/shard_map/ppermute | solution.py:18
  12.5 651.6 %all-reduce.8.cloned.1.call-start = ((), (), s32[]{:S(2)}) async-start(), calls=%async_computation.12 | async-start | bytes 8388608 | tf_op jit(solution)/shard_map/psum | solution.py:263
  38.7 37.9 %copy-start.50 = (f32[8,1,256]{2,1,0:T(1,128)}, f32[8,1,256]{2,1,0:T(1,128)S(1)}, u32[]{:S(2)}) copy-start(f32[8,1,256]{2,1,0:T(1,128)S(1)} %convert_element_type.136) | copy-start | bytes 24580
  41.5 35.2 %copy-start.56 = (f32[1,2,2,128]{3,1,2,0:T(2,128)}, f32[1,2,2,128]{3,1,2,0:T(2,128)S(1)}, u32[]{:S(2)}) copy-start(f32[1,2,2,128]{3,1,2,0:T(2,128)S(1)} %copy.103) | copy-start | bytes 6148
  41.5 35.2 %copy-start.58 = (f32[1,2,2,128]{3,1,2,0:T(2,128)}, f32[1,2,2,128]{3,1,2,0:T(2,128)S(1)}, u32[]{:S(2)}) copy-start(f32[1,2,2,128]{3,1,2,0:T(2,128)S(1)} %copy.102) | copy-start | bytes 6148
  41.7 33.3 %collective-permute-start.3 = (bf16[512,864]{0,1:T(8,128)(2,1)S(1)}, bf16[512,864]{0,1:T(8,128)(2,1)S(1)}, u32[]{:S(2)}, u32[]{:S(2)}) collective-permute-start(bf16[512,864]{0,1:T(8,128)(2,1)S(1)} %maximum_select_fusion.2), channel_id=1, source_target_pairs={{0,8},{4,12},{8,0},{12,4},{16,24},{20,28},{24,16},{28,20},{1,9},{5... | collective-permute-start | bytes 2654216 | tf_op jit(solution)/shard_map/ppermute | solution.py:18
  42.6 33.1 %copy-start.67 = (f32[2]{0:T(128)S(1)}, f32[2]{0:T(128)}, u32[]{:S(2)}) copy-start(f32[2]{0:T(128)} %param.29) | copy-start | bytes 28
  75.6 83.3 %collective-permute-start.4 = (bf16[1024,864]{0,1:T(8,128)(2,1)S(1)}, bf16[1024,864]{0,1:T(8,128)(2,1)S(1)}, u32[]{:S(2)}, u32[]{:S(2)}) collective-permute-start(bf16[1024,864]{0,1:T(8,128)(2,1)S(1)} %maximum_select_fusion.1), channel_id=1, source_target_pairs={{0,16},{4,20},{8,24},{12,28},{16,0},{20,4},{24,8},{28,12},{1,17},{... | collective-permute-start | bytes 5308424 | tf_op jit(solution)/shard_map/ppermute | solution.py:18
  75.7 119.1 %copy-start.63 = (f32[256,2]{0,1:T(2,128)}, f32[256,2]{0,1:T(2,128)S(1)}, u32[]{:S(2)}) copy-start(f32[256,2]{0,1:T(2,128)S(1)} %get-tuple-element.128) | copy-start | bytes 6148
  75.8 479.5 %copy-start.65 = (f32[256,2]{0,1:T(2,128)}, f32[256,2]{0,1:T(2,128)S(1)}, u32[]{:S(2)}) copy-start(f32[256,2]{0,1:T(2,128)S(1)} %get-tuple-element.127) | copy-start | bytes 6148
  75.9 116.9 %copy-start.33 = (f32[2,256,256]{2,1,0:T(8,128)}, f32[2,256,256]{2,1,0:T(8,128)S(1)}, u32[]{:S(2)}) copy-start(f32[2,256,256]{2,1,0:T(8,128)S(1)} %exponential_select_fusion) | copy-start | bytes 1572868
  76.6 83.8 %copy-start.7 = (bf16[2,256,2048]{2,1,0:T(8,128)(2,1)}, bf16[2,256,2048]{2,1,0:T(8,128)(2,1)S(1)}, u32[]{:S(2)}) copy-start(bf16[2,256,2048]{2,1,0:T(8,128)(2,1)S(1)} %fusion.4) | copy-start | bytes 6291460
  162.5 30.7 %copy-start.15 = (bf16[2,256,2,432]{1,3,2,0:T(8,128)(2,1)}, bf16[2,256,2,432]{1,3,2,0:T(8,128)(2,1)S(1)}, u32[]{:S(2)}) copy-start(bf16[2,256,2,432]{1,3,2,0:T(8,128)(2,1)S(1)} %fusion.27) | copy-start | bytes 2654212
  198.7 55.5 %collective-permute-start = (f32[2,2,256,432]{2,3,1,0:T(8,128)}, f32[2,2,256,432]{2,3,1,0:T(8,128)S(1)}, u32[]{:S(2)}, u32[]{:S(2)}) collective-permute-start(f32[2,2,256,432]{2,3,1,0:T(8,128)} %multiply_add_fusion.5), channel_id=1, source_target_pairs={{0,4},{4,8},{8,12},{12,16},{16,20},{20,24},{24,28},{1,5},{5,9},{9,... | collective-permute-start | bytes 5308424 | tf_op jit(solution)/shard_map/while/body/eval_jaxpr/ppermute | solution.py:29
  255.7 61.9 %collective-permute-start = (f32[2,2,256,432]{2,3,1,0:T(8,128)}, f32[2,2,256,432]{2,3,1,0:T(8,128)S(1)}, u32[]{:S(2)}, u32[]{:S(2)}) collective-permute-start(f32[2,2,256,432]{2,3,1,0:T(8,128)} %multiply_add_fusion.5), channel_id=1, source_target_pairs={{0,4},{4,8},{8,12},{12,16},{16,20},{20,24},{24,28},{1,5},{5,9},{9,... | collective-permute-start | bytes 5308424 | tf_op jit(solution)/shard_map/while/body/eval_jaxpr/ppermute | solution.py:29
  319.1 63.2 %collective-permute-start = (f32[2,2,256,432]{2,3,1,0:T(8,128)}, f32[2,2,256,432]{2,3,1,0:T(8,128)S(1)}, u32[]{:S(2)}, u32[]{:S(2)}) collective-permute-start(f32[2,2,256,432]{2,3,1,0:T(8,128)} %multiply_add_fusion.5), channel_id=1, source_target_pairs={{0,4},{4,8},{8,12},{12,16},{16,20},{20,24},{24,28},{1,5},{5,9},{9,... | collective-permute-start | bytes 5308424 | tf_op jit(solution)/shard_map/while/body/eval_jaxpr/ppermute | solution.py:29
  383.8 51.2 %collective-permute-start = (f32[2,2,256,432]{2,3,1,0:T(8,128)}, f32[2,2,256,432]{2,3,1,0:T(8,128)S(1)}, u32[]{:S(2)}, u32[]{:S(2)}) collective-permute-start(f32[2,2,256,432]{2,3,1,0:T(8,128)} %multiply_add_fusion.5), channel_id=1, source_target_pairs={{0,4},{4,8},{8,12},{12,16},{16,20},{20,24},{24,28},{1,5},{5,9},{9,... | collective-permute-start | bytes 5308424 | tf_op jit(solution)/shard_map/while/body/eval_jaxpr/ppermute | solution.py:29
  436.5 39.2 %collective-permute-start = (f32[2,2,256,432]{2,3,1,0:T(8,128)}, f32[2,2,256,432]{2,3,1,0:T(8,128)S(1)}, u32[]{:S(2)}, u32[]{:S(2)}) collective-permute-start(f32[2,2,256,432]{2,3,1,0:T(8,128)} %multiply_add_fusion.5), channel_id=1, source_target_pairs={{0,4},{4,8},{8,12},{12,16},{16,20},{20,24},{24,28},{1,5},{5,9},{9,... | collective-permute-start | bytes 5308424 | tf_op jit(solution)/shard_map/while/body/eval_jaxpr/ppermute | solution.py:29
  477.3 38.4 %collective-permute-start = (f32[2,2,256,432]{2,3,1,0:T(8,128)}, f32[2,2,256,432]{2,3,1,0:T(8,128)S(1)}, u32[]{:S(2)}, u32[]{:S(2)}) collective-permute-start(f32[2,2,256,432]{2,3,1,0:T(8,128)} %multiply_add_fusion.5), channel_id=1, source_target_pairs={{0,4},{4,8},{8,12},{12,16},{16,20},{20,24},{24,28},{1,5},{5,9},{9,... | collective-permute-start | bytes 5308424 | tf_op jit(solution)/shard_map/while/body/eval_jaxpr/ppermute | solution.py:29
  517.2 37.5 %collective-permute-start = (f32[2,2,256,432]{2,3,1,0:T(8,128)}, f32[2,2,256,432]{2,3,1,0:T(8,128)S(1)}, u32[]{:S(2)}, u32[]{:S(2)}) collective-permute-start(f32[2,2,256,432]{2,3,1,0:T(8,128)} %multiply_add_fusion.5), channel_id=1, source_target_pairs={{0,4},{4,8},{8,12},{12,16},{16,20},{20,24},{24,28},{1,5},{5,9},{9,... | collective-permute-start | bytes 5308424 | tf_op jit(solution)/shard_map/while/body/eval_jaxpr/ppermute | solution.py:29
  575.4 158.0 %all-gather.19.cloned.1.call-start = ((), (), s32[]{:S(2)}) async-start(), calls=%async_computation.13 | async-start | bytes 3981312 | tf_op jit(solution)/shard_map/all_gather | solution.py:211
  576.0 224.8 %all-gather.21.cloned.1.call-start = ((), (), s32[]{:S(2)}) async-start(), calls=%async_computation.14 | async-start | bytes 3981312 | tf_op jit(solution)/shard_map/all_gather | solution.py:212
  576.7 291.5 %all-gather.23.cloned.1.call-start = ((), (), s32[]{:S(2)}) async-start(), calls=%async_computation.15 | async-start | bytes 3981312 | tf_op jit(solution)/shard_map/all_gather | solution.py:213
  577.5 389.1 %all-reduce.10.cloned.1.call-start = ((), (), s32[]{:S(2)}) async-start(), calls=%async_computation.16 | async-start | bytes 8388608 | tf_op jit(solution)/shard_map/psum | solution.py:305
  868.2 7.4 copy-start.24
  882.8 463.9 %all-gather.25.cloned.1.call-start = ((), (), s32[]{:S(2)}) async-start(), calls=%async_computation.17 | async-start | bytes 3981312 | tf_op jit(solution)/shard_map/all_gather | solution.py:277
  883.4 625.2 %all-reduce.12.cloned.1.call-start = ((), (), s32[]{:S(2)}) async-start(), calls=%async_computation.26 | async-start | bytes 16777216 | tf_op jit(solution)/shard_map/psum | solution.py:271
  966.6 5.3 copy-start.1
  966.6 5.9 copy-start.13
  966.6 5.9 copy-start.53
  966.6 6.0 copy-start.61
  975.9 4.6 copy-start.4
  996.8 325.6 %copy-start.64 = (f32[256,2]{0,1:T(2,128)S(1)}, f32[256,2]{0,1:T(2,128)}, u32[]{:S(2)}) copy-start(f32[256,2]{0,1:T(2,128)} %copy-done.63) | copy-start | bytes 6148
  998.3 61.0 %collective-permute-start.1 = (f32[2,2,256,432]{2,3,1,0:T(8,128)}, f32[2,2,256,432]{2,3,1,0:T(8,128)S(1)}, u32[]{:S(2)}, u32[]{:S(2)}) collective-permute-start(f32[2,2,256,432]{2,3,1,0:T(8,128)} %multiply_add_fusion.6), channel_id=1, source_target_pairs={{4,0},{8,4},{12,8},{16,12},{20,16},{24,20},{28,24},{5,1},{9,5},{13... | collective-permute-start | bytes 5308424 | tf_op jit(solution)/shard_map/while/body/eval_jaxpr/ppermute | solution.py:29
  1060.8 52.1 %collective-permute-start.1 = (f32[2,2,256,432]{2,3,1,0:T(8,128)}, f32[2,2,256,432]{2,3,1,0:T(8,128)S(1)}, u32[]{:S(2)}, u32[]{:S(2)}) collective-permute-start(f32[2,2,256,432]{2,3,1,0:T(8,128)} %multiply_add_fusion.6), channel_id=1, source_target_pairs={{4,0},{8,4},{12,8},{16,12},{20,16},{24,20},{28,24},{5,1},{9,5},{13... | collective-permute-start | bytes 5308424 | tf_op jit(solution)/shard_map/while/body/eval_jaxpr/ppermute | solution.py:29
  1114.5 42.0 %collective-permute-start.1 = (f32[2,2,256,432]{2,3,1,0:T(8,128)}, f32[2,2,256,432]{2,3,1,0:T(8,128)S(1)}, u32[]{:S(2)}, u32[]{:S(2)}) collective-permute-start(f32[2,2,256,432]{2,3,1,0:T(8,128)} %multiply_add_fusion.6), channel_id=1, source_target_pairs={{4,0},{8,4},{12,8},{16,12},{20,16},{24,20},{28,24},{5,1},{9,5},{13... | collective-permute-start | bytes 5308424 | tf_op jit(solution)/shard_map/while/body/eval_jaxpr/ppermute | solution.py:29
  1158.0 41.2 %collective-permute-start.1 = (f32[2,2,256,432]{2,3,1,0:T(8,128)}, f32[2,2,256,432]{2,3,1,0:T(8,128)S(1)}, u32[]{:S(2)}, u32[]{:S(2)}) collective-permute-start(f32[2,2,256,432]{2,3,1,0:T(8,128)} %multiply_add_fusion.6), channel_id=1, source_target_pairs={{4,0},{8,4},{12,8},{16,12},{20,16},{24,20},{28,24},{5,1},{9,5},{13... | collective-permute-start | bytes 5308424 | tf_op jit(solution)/shard_map/while/body/eval_jaxpr/ppermute | solution.py:29
  1200.7 40.3 %collective-permute-start.1 = (f32[2,2,256,432]{2,3,1,0:T(8,128)}, f32[2,2,256,432]{2,3,1,0:T(8,128)S(1)}, u32[]{:S(2)}, u32[]{:S(2)}) collective-permute-start(f32[2,2,256,432]{2,3,1,0:T(8,128)} %multiply_add_fusion.6), channel_id=1, source_target_pairs={{4,0},{8,4},{12,8},{16,12},{20,16},{24,20},{28,24},{5,1},{9,5},{13... | collective-permute-start | bytes 5308424 | tf_op jit(solution)/shard_map/while/body/eval_jaxpr/ppermute | solution.py:29
  1242.6 39.5 %collective-permute-start.1 = (f32[2,2,256,432]{2,3,1,0:T(8,128)}, f32[2,2,256,432]{2,3,1,0:T(8,128)S(1)}, u32[]{:S(2)}, u32[]{:S(2)}) collective-permute-start(f32[2,2,256,432]{2,3,1,0:T(8,128)} %multiply_add_fusion.6), channel_id=1, source_target_pairs={{4,0},{8,4},{12,8},{16,12},{20,16},{24,20},{28,24},{5,1},{9,5},{13... | collective-permute-start | bytes 5308424 | tf_op jit(solution)/shard_map/while/body/eval_jaxpr/ppermute | solution.py:29
  1283.6 38.6 %collective-permute-start.1 = (f32[2,2,256,432]{2,3,1,0:T(8,128)}, f32[2,2,256,432]{2,3,1,0:T(8,128)S(1)}, u32[]{:S(2)}, u32[]{:S(2)}) collective-permute-start(f32[2,2,256,432]{2,3,1,0:T(8,128)} %multiply_add_fusion.6), channel_id=1, source_target_pairs={{4,0},{8,4},{12,8},{16,12},{20,16},{24,20},{28,24},{5,1},{9,5},{13... | collective-permute-start | bytes 5308424 | tf_op jit(solution)/shard_map/while/body/eval_jaxpr/ppermute | solution.py:29
  1328.6 6.2 copy-start.11
  1338.5 8.2 copy-start.29
  1346.7 4.6 copy-start.12
  1346.7 5.1 copy-start.26
  1346.7 5.1 copy-start.31
  1355.3 246.1 %reduce-scatter.11.cloned.1.call-start = ((), (), s32[]{:S(2)}) async-start(), calls=%async_computation.19 | async-start | bytes 4718592 | tf_op jit(solution)/shard_map/reduce_scatter | solution.py:366
  1360.2 333.4 %reduce-scatter.9.cloned.1.call-start = ((), (), s32[]{:S(2)}) async-start(), calls=%async_computation.18 | async-start | bytes 4718592 | tf_op jit(solution)/shard_map/reduce_scatter | solution.py:365
  1363.7 463.3 %reduce-scatter.19.cloned.1.call-start = ((), (), s32[]{:S(2)}) async-start(), calls=%async_computation.23 | async-start | bytes 7962624 | tf_op jit(solution)/shard_map/reduce_scatter | solution.py:370
  1371.2 588.5 %reduce-scatter.21.cloned.1.call-start = ((), (), s32[]{:S(2)}) async-start(), calls=%async_computation.24 | async-start | bytes 7962624 | tf_op jit(solution)/shard_map/reduce_scatter | solution.py:371
  1378.9 713.6 %reduce-scatter.23.cloned.1.call-start = ((), (), s32[]{:S(2)}) async-start(), calls=%async_computation.25 | async-start | bytes 7962624 | tf_op jit(solution)/shard_map/reduce_scatter | solution.py:372
  1386.6 838.8 %reduce-scatter.17.cloned.1.call-start = ((), (), s32[]{:S(2)}) async-start(), calls=%async_computation.22 | async-start | bytes 7962624 | tf_op jit(solution)/shard_map/reduce_scatter | solution.py:369
  1394.8 963.4 %reduce-scatter.13.cloned.1.call-start = ((), (), s32[]{:S(2)}) async-start(), calls=%async_computation.20 | async-start | bytes 7962624 | tf_op jit(solution)/shard_map/reduce_scatter | solution.py:367
  1401.1 1090.1 %reduce-scatter.15.cloned.1.call-start = ((), (), s32[]{:S(2)}) async-start(), calls=%async_computation.21 | async-start | bytes 7962624 | tf_op jit(solution)/shard_map/reduce_scatter | solution.py:368
  1407.8 100.7 %copy-start.3 = (bf16[2,256,2048]{2,1,0:T(8,128)(2,1)S(1)}, bf16[2,256,2048]{2,1,0:T(8,128)(2,1)}, u32[]{:S(2)}) copy-start(bf16[2,256,2048]{2,1,0:T(8,128)(2,1)} %param.17) | copy-start | bytes 6291460
  1407.8 100.7 %copy-start.51 = (f32[8,1,256]{2,1,0:T(1,128)S(1)}, f32[8,1,256]{2,1,0:T(1,128)}, u32[]{:S(2)}) copy-start(f32[8,1,256]{2,1,0:T(1,128)} %copy-done.50) | copy-start | bytes 24580
  1407.8 100.7 %copy-start.57 = (f32[1,2,2,128]{3,1,2,0:T(2,128)S(1)}, f32[1,2,2,128]{3,1,2,0:T(2,128)}, u32[]{:S(2)}) copy-start(f32[1,2,2,128]{3,1,2,0:T(2,128)} %copy-done.56) | copy-start | bytes 6148
  1407.9 100.7 %copy-start.59 = (f32[1,2,2,128]{3,1,2,0:T(2,128)S(1)}, f32[1,2,2,128]{3,1,2,0:T(2,128)}, u32[]{:S(2)}) copy-start(f32[1,2,2,128]{3,1,2,0:T(2,128)} %copy-done.58) | copy-start | bytes 6148
  1551.7 5.7 copy-start.5
  1551.8 6.9 copy-start.14
  (43 other events, 99.5 us)
Sparse Core Ops, SparseCore 0:
  10.1 60.8 all-gather.14
  73.2 111.2 all-gather.12
  186.5 88.5 all-gather.10
  277.0 94.9 all-gather.16
  575.5 88.5 all-reduce.7
  666.0 67.2 all-gather.18
  735.4 65.3 all-gather.20
  802.8 65.3 all-gather.22
  882.9 83.6 all-reduce.9
  968.5 91.6 all-gather.24
  1355.4 153.0 all-reduce.11
  1512.6 88.8 reduce-scatter.10
  1605.6 87.9 reduce-scatter.8
  1697.7 129.1 reduce-scatter.18
  1831.1 128.6 reduce-scatter.20
  1963.9 128.6 reduce-scatter.22
  2096.7 128.6 reduce-scatter.16
  2229.5 128.6 reduce-scatter.12
  2362.5 128.6 reduce-scatter.14
